TPU v7x, 16 devices: a 4x2x1 block of a 4x4x8 slice. The times are simulated.
16 devices in a mesh: lev: 2 (over y, z), w: 8 (over x, core).
Axes of the slice: x: 4, y: 2, z: 1, core: 2. Of those that a mesh axis runs over, the one named last changes fastest.
The devices are a block of a 4x4x8 slice.
Arguments:
- coef: float32 [160, 2, 256, 160], P('w', None, 'lev'), parts along dimension 2
- legendre: float32 [160, 160, 160], replicated
- gauss_weight: float32 [160], replicated
Outputs:
- output 1: float32 [256, 160, 320], P('lev', 'w'), parts along dimension 0
- output 2: float32 [160, 2, 256, 160], P('w', None, 'lev'), parts along dimension 2
There are 2 independent parts. A program takes and returns all parts, laid end to end along the dimension named above; an argument that names none is the same for every part.
All inputs are finite; a program needn't handle non-finite values.
Results may differ from a plain program's by a relative error of at most 0.001.
Values sent between devices are 32-bit elements.
A program may use at most 768 MiB of HBM per device.

v0:
```python
import functools

import jax
import jax.numpy as jnp
import ml_dtypes
import numpy as np
from jax import lax
from jax.experimental import pallas as pl
from jax.experimental.pallas import tpu as pltpu
from jax.sharding import PartitionSpec as P

MESH = pl.DeviceIdType.MESH
F32, BF16 = jnp.float32, jnp.bfloat16
LANES = 128
SUB = 8
QUAD = 4
GROUPS = 4


def split_np(mat):
    hi = mat.astype(np.float32).astype(ml_dtypes.bfloat16)
    lo = (mat - hi.astype(np.float64)).astype(np.float32).astype(ml_dtypes.bfloat16)
    return hi, lo


def fourier_matrices(waves):
    lon = 2 * waves
    m = np.arange(waves)[:, None]
    n = np.arange(lon)[None, :]
    ang = 2.0 * np.pi * ((m * n) % lon) / lon
    fwd = np.concatenate([np.cos(ang), -np.sin(ang)], axis=0)
    scale = np.where(np.arange(waves) == 0, 1.0, 2.0) / lon
    inv = (fwd * np.tile(scale, 2)[:, None]).T
    out = []
    for mat in (inv, fwd):
        hi, lo = split_np(mat)
        out.append(np.concatenate([hi, hi, lo], axis=1))
    return out


def split(x):
    hi = x.astype(BF16)
    lo = (x - hi.astype(F32)).astype(BF16)
    return hi, lo


def dot(a, b, dims=((1,), (0,))):
    return lax.dot_general(a, b, (dims, ((), ())), preferred_element_type=F32)


def kernel(dims, coef_hbm, leg_hbm, inv_hbm, fwd_hbm, wt_ref, grid_hbm, spec_hbm,
           coef, leg, inv, fwd, send_a, recv_a, send_b, recv_b, grid, spec,
           load_sem, mat_sem, send_sem_a, recv_sem_a, send_sem_b, recv_sem_b, last_sem, out_sem, grid_sem):
    group, wave_loc, levels, degs, lat_loc, lat_pad, waves, lon = dims
    chunks = lat_loc // QUAD
    planes = -(-lon // LANES)
    per_group = wave_loc // GROUPS
    msg = wave_loc * SUB
    part = per_group * SUB
    me = lax.axis_index('w')

    barrier = pltpu.get_barrier_semaphore()
    for off in range(1, group):
        pl.semaphore_signal(barrier, inc=1, device_id={'w': lax.rem(me + off, group)}, device_id_type=MESH)

    loads = []
    for g in range(GROUPS):
        own = pl.ds(g * per_group, per_group)
        first = pltpu.make_async_copy(coef_hbm.at[own], coef.at[own], load_sem.at[0, g])
        second = pltpu.make_async_copy(leg_hbm.at[pl.ds(me * wave_loc + g * per_group, per_group)], leg.at[own], load_sem.at[1, g])
        first.start()
        second.start()
        loads.append((first, second))
    mats = [pltpu.make_async_copy(inv_hbm, inv, mat_sem.at[0]), pltpu.make_async_copy(fwd_hbm, fwd, mat_sem.at[1])]
    for copy in mats:
        copy.start()

    low = lax.broadcasted_iota(jnp.int32, (SUB, levels), 0) < QUAD

    def rows(start, size):
        return pl.ds(pl.multiple_of(start, SUB), size)

    def copy_a(off, c, start, size):
        dst = lax.rem(me + off, group)
        return pltpu.make_async_remote_copy(
            src_ref=send_a.at[rows((dst * chunks + c) * msg + start, size)],
            dst_ref=recv_a.at[rows((c * group + me) * msg + start, size)],
            send_sem=send_sem_a, recv_sem=recv_sem_a.at[c], device_id={'w': dst}, device_id_type=MESH)

    def copy_b(off, c, start, size, sem):
        dst = lax.rem(me + off, group)
        return pltpu.make_async_remote_copy(
            src_ref=send_b.at[rows((c * group + dst) * msg + start, size)],
            dst_ref=recv_b.at[rows((c * group + me) * msg + start, size)],
            send_sem=send_sem_b, recv_sem=sem, device_id={'w': dst}, device_id_type=MESH)

    order = [group // 2, 2, group - 2, group // 2 + 1, 3, group - 1, 1]
    order = order if sorted(order) == list(range(1, group)) else list(range(1, group))

    for g in range(GROUPS):
        for copy in loads[g]:
            copy.wait()

        def legendre_body(i, carry):
            m = g * per_group + i
            leg_hi, leg_lo = split(jnp.transpose(leg[m]))
            c_hi, c_lo = split(coef[m].reshape(2 * levels, degs))
            nt = ((1,), (1,))
            f = dot(leg_hi, c_hi, nt) + dot(leg_lo, c_hi, nt) + dot(leg_hi, c_lo, nt)
            for t in range(group * lat_loc // SUB):
                re = f[t * SUB:(t + 1) * SUB, :levels]
                im = f[t * SUB:(t + 1) * SUB, levels:]
                send_a[rows((2 * t * wave_loc + m) * SUB, SUB), :] = jnp.where(low, re, pltpu.roll(im, QUAD, 0))
                send_a[rows(((2 * t + 1) * wave_loc + m) * SUB, SUB), :] = jnp.where(low, pltpu.roll(re, QUAD, 0), im)
            return carry

        lax.fori_loop(0, per_group, legendre_body, 0)
        if g == 0:
            pl.semaphore_wait(barrier, group - 1)
        for off in order:
            copy_a(off, 0, g * part, part).start()

    @pl.loop(1, chunks)
    def _(c):
        for off in order:
            copy_a(off, c, 0, msg).start()

    @pl.loop(0, chunks)
    def _(c):
        recv_a[rows((c * group + me) * msg, msg), :] = send_a[rows((me * chunks + c) * msg, msg), :]

    for copy in mats:
        copy.wait()

    @pl.loop(0, chunks)
    def _(c):
        landed = recv_a.at[pl.ds(0, (group - 1) * msg)]
        pltpu.make_async_copy(landed, landed, recv_sem_a.at[c]).wait()

        @pl.loop(0, QUAD // 2)
        def _(pair):
            halves = []
            for u in range(2):
                row = c * (group * msg) + 2 * pair + u
                re = recv_a[pl.ds(row, waves, stride=SUB), :]
                im = recv_a[pl.ds(row + QUAD, waves, stride=SUB), :]
                halves.append(jnp.concatenate([re, im], axis=0))
            f_hi, f_lo = split(jnp.concatenate(halves, axis=1))
            g_val = dot(inv[...], jnp.concatenate([f_hi, f_lo, f_hi], axis=0))
            for u in range(2):
                j = c * QUAD + 2 * pair + u
                for p in range(planes):
                    piece = g_val[p * LANES:min((p + 1) * LANES, lon), u * levels:(u + 1) * levels]
                    if piece.shape[0] < LANES:
                        piece = jnp.concatenate([piece, jnp.zeros((LANES - piece.shape[0], levels), F32)], axis=0)
                    grid[pl.ds(p * levels * lat_pad + j, levels, stride=lat_pad), :] = jnp.transpose(piece)
            q_hi, q_lo = split(g_val * g_val)
            h = dot(fwd[...], jnp.concatenate([q_hi, q_lo, q_hi], axis=0))
            for u in range(2):
                row = c * (group * msg) + 2 * pair + u
                hw = h[:, u * levels:(u + 1) * levels] * wt_ref[me * lat_loc + c * QUAD + 2 * pair + u]
                send_b[pl.ds(row, waves, stride=SUB), :] = hw[:waves]
                send_b[pl.ds(row + QUAD, waves, stride=SUB), :] = hw[waves:]

        @pl.when(c < chunks - 1)
        def _():
            for off in order:
                copy_b(off, c, 0, msg, recv_sem_b).start()

        @pl.when(c == chunks - 1)
        def _():
            for g in range(GROUPS):
                for off in order:
                    copy_b(off, c, g * part, part, last_sem.at[g]).start()

        recv_b[rows((c * group + me) * msg, msg), :] = send_b[rows((c * group + me) * msg, msg), :]

    grid_out = []
    for p in range(planes):
        copy = pltpu.make_async_copy(grid.at[pl.ds(p * levels * lat_pad, levels * lat_pad)], grid_hbm.at[:, pl.ds(p * LANES, LANES)], grid_sem.at[p])
        copy.start()
        grid_out.append(copy)

    landed = recv_b.at[pl.ds(0, (chunks - 1) * (group - 1) * msg)]
    pltpu.make_async_copy(landed, landed, recv_sem_b).wait()
    outs = []
    for g in range(GROUPS):
        landed = recv_b.at[pl.ds(0, (group - 1) * part)]
        pltpu.make_async_copy(landed, landed, last_sem.at[g]).wait()

        def back_body(i, carry):
            m = g * per_group + i
            re, im = [], []
            for t in range(group * lat_loc // SUB):
                tiles = []
                for q in (2 * t, 2 * t + 1):
                    s, c = divmod(q, chunks)
                    tiles.append(recv_b[rows(((c * group + s) * wave_loc + m) * SUB, SUB), :])
                a, b = tiles
                re.append(jnp.where(low, a, pltpu.roll(b, QUAD, 0)))
                im.append(jnp.where(low, pltpu.roll(a, QUAD, 0), b))
            h_hi, h_lo = split(jnp.concatenate([jnp.concatenate(re, axis=0), jnp.concatenate(im, axis=0)], axis=1))
            leg_hi, leg_lo = split(leg[m])
            s_val = dot(leg_hi, h_hi) + dot(leg_lo, h_hi) + dot(leg_hi, h_lo)
            spec[m] = jnp.transpose(s_val).reshape(2, levels, degs)
            return carry

        lax.fori_loop(0, per_group, back_body, 0)
        own = pl.ds(g * per_group, per_group)
        copy = pltpu.make_async_copy(spec.at[own], spec_hbm.at[own], out_sem.at[g])
        copy.start()
        outs.append(copy)

    for copy in outs:
        copy.wait()
    for copy in grid_out:
        copy.wait()
    sent = send_a.at[pl.ds(0, (group - 1) * chunks * msg)]
    pltpu.make_async_copy(sent, sent, send_sem_a).wait()
    pltpu.make_async_copy(sent, sent, send_sem_b).wait()


def solution(mesh):
    group = mesh.shape['w']

    def per_device(coef, legendre, gauss_weight):
        wave_loc, _, levels, degs = coef.shape
        waves = wave_loc * group
        lon = 2 * waves
        lat_loc = legendre.shape[2] // group
        lat_pad = -(-lat_loc // SUB) * SUB
        inv, fwd = (jnp.asarray(x) for x in fourier_matrices(waves))
        planes = -(-lon // LANES)
        total = group * lat_loc // QUAD * wave_loc * SUB
        dims = (group, wave_loc, levels, degs, lat_loc, lat_pad, waves, lon)
        hbm = pl.BlockSpec(memory_space=pl.ANY)
        dma = pltpu.SemaphoreType.DMA
        grid, spec = pl.pallas_call(
            functools.partial(kernel, dims),
            out_shape=(jax.ShapeDtypeStruct((levels * lat_pad, planes * LANES), F32), jax.ShapeDtypeStruct(coef.shape, F32)),
            in_specs=[hbm, hbm, hbm, hbm, pl.BlockSpec(memory_space=pltpu.SMEM)],
            out_specs=(hbm, hbm),
            scratch_shapes=[
                pltpu.VMEM(coef.shape, F32),
                pltpu.VMEM((wave_loc, degs, legendre.shape[2]), F32),
                pltpu.VMEM(inv.shape, BF16),
                pltpu.VMEM(fwd.shape, BF16),
                pltpu.VMEM((total, levels), F32),
                pltpu.VMEM((total, levels), F32),
                pltpu.VMEM((total, levels), F32),
                pltpu.VMEM((total, levels), F32),
                pltpu.VMEM((planes * levels * lat_pad, LANES), F32),
                pltpu.VMEM(coef.shape, F32),
                dma((2, GROUPS)), dma((2,)), dma, dma((lat_loc // QUAD,)), dma, dma, dma((GROUPS,)), dma((GROUPS,)), dma((planes,)),
            ],
            compiler_params=pltpu.CompilerParams(collective_id=0, has_side_effects=True, vmem_limit_bytes=56 * 2**20),
            name='transform_pair',
        )(coef, legendre, inv, fwd, gauss_weight)
        return grid.reshape(levels, lat_pad, planes * LANES)[:, :lat_loc, :lon], spec

    return jax.shard_map(per_device, mesh=mesh, in_specs=(P('w', None, 'lev', None), P(None, None, None), P(None)), out_specs=(P('lev', 'w', None), P('w', None, 'lev', None)), check_vma=False)
```

profile of v0, /device:TPU:113, one launch (start us, length us, event | category | flops | bytes accessed | tf_op | source)
XLA Modules:
  0.0 100.0 jit_solution(2755818188638160811)
XLA Ops:
  0.6 5.4 %copy.7.coef_hbm = f32[20,2,128,160]{3,2,1,0:T(8,128)} copy(f32[20,2,128,160]{2,3,1,0:T(8,128)} %param.5) | data formatting | bytes 6553600 | tf_op args[0]
  6.1 82.6 %transform_pair.1 = (f32[3072,384]{1,0:T(8,128)}, f32[20,2,128,160]{3,2,1,0:T(8,128)}) custom-call(f32[20,2,128,160]{3,2,1,0:T(8,128)} %copy.7.coef_hbm, f32[160,160,160]{2,1,0:T(8,128)} %leg_hbm.1, bf16[320,960]{1,0:T(8,128)(2,1)} %constant.4.clone.inv_hbm, bf16[320,960]{1,0:T(8,128)(2,1)} %constant.5.clone.fwd_hbm, f32[160]{0:T(256)} %wt_ref.1), custom_call_target="tpu_custom_call" | custom-call | tf_op jit(solution)/shard_map/transform_pair/pallas_call | solution.py:238
  88.7 5.5 %copy.10 = f32[128,20,320]{0,2,1:T(8,128)} copy(f32[128,20,320]{2,1,0:T(8,128)} %bitcast.2) | data formatting | bytes 6553600
  94.2 5.8 %copy.9 = f32[20,2,128,160]{2,3,1,0:T(8,128)} copy(f32[20,2,128,160]{3,2,1,0:T(8,128)} %get-tuple-element.7) | data formatting | bytes 6553600
where the time goes:
time: 100 us
  Pallas kernels  82.6 us (83%)
  local copies, waits for them, and re-layouts  16.7 us (17%)
    pallas_call x1, Pallas kernels, per_device(): pl.pallas_call(functools.partial(kernel, dims), out_shape=(jax.ShapeDtype...  82.6 us
    unnamed x3, local copies, waits for them, and re-layouts  16.7 us

commit v1 on v0

--- a/solution.py
+++ b/solution.py
@@ -11,7 +11,6 @@
 
 MESH = pl.DeviceIdType.MESH
 F32, BF16 = jnp.float32, jnp.bfloat16
-LANES = 128
 SUB = 8
 QUAD = 4
 GROUPS = 4
@@ -51,9 +50,8 @@
 def kernel(dims, coef_hbm, leg_hbm, inv_hbm, fwd_hbm, wt_ref, grid_hbm, spec_hbm,
            coef, leg, inv, fwd, send_a, recv_a, send_b, recv_b, grid, spec,
            load_sem, mat_sem, send_sem_a, recv_sem_a, send_sem_b, recv_sem_b, last_sem, out_sem, grid_sem):
-    group, wave_loc, levels, degs, lat_loc, lat_pad, waves, lon = dims
+    group, wave_loc, levels, degs, lat_loc, waves, lon = dims
     chunks = lat_loc // QUAD
-    planes = -(-lon // LANES)
     per_group = wave_loc // GROUPS
     msg = wave_loc * SUB
     part = per_group * SUB
@@ -104,9 +102,8 @@
         def legendre_body(i, carry):
             m = g * per_group + i
             leg_hi, leg_lo = split(jnp.transpose(leg[m]))
-            c_hi, c_lo = split(coef[m].reshape(2 * levels, degs))
-            nt = ((1,), (1,))
-            f = dot(leg_hi, c_hi, nt) + dot(leg_lo, c_hi, nt) + dot(leg_hi, c_lo, nt)
+            c_hi, c_lo = split(jnp.concatenate([coef[m, 0], coef[m, 1]], axis=1))
+            f = dot(leg_hi, c_hi) + dot(leg_lo, c_hi) + dot(leg_hi, c_lo)
             for t in range(group * lat_loc // SUB):
                 re = f[t * SUB:(t + 1) * SUB, :levels]
                 im = f[t * SUB:(t + 1) * SUB, levels:]
@@ -148,12 +145,7 @@
             f_hi, f_lo = split(jnp.concatenate(halves, axis=1))
             g_val = dot(inv[...], jnp.concatenate([f_hi, f_lo, f_hi], axis=0))
             for u in range(2):
-                j = c * QUAD + 2 * pair + u
-                for p in range(planes):
-                    piece = g_val[p * LANES:min((p + 1) * LANES, lon), u * levels:(u + 1) * levels]
-                    if piece.shape[0] < LANES:
-                        piece = jnp.concatenate([piece, jnp.zeros((LANES - piece.shape[0], levels), F32)], axis=0)
-                    grid[pl.ds(p * levels * lat_pad + j, levels, stride=lat_pad), :] = jnp.transpose(piece)
+                grid[c * QUAD + 2 * pair + u] = g_val[:, u * levels:(u + 1) * levels]
             q_hi, q_lo = split(g_val * g_val)
             h = dot(fwd[...], jnp.concatenate([q_hi, q_lo, q_hi], axis=0))
             for u in range(2):
@@ -173,13 +165,9 @@
                 for off in order:
                     copy_b(off, c, g * part, part, last_sem.at[g]).start()
 
+        lats = pl.ds(c * QUAD, QUAD)
+        pltpu.make_async_copy(grid.at[lats], grid_hbm.at[lats], grid_sem).start()
         recv_b[rows((c * group + me) * msg, msg), :] = send_b[rows((c * group + me) * msg, msg), :]
-
-    grid_out = []
-    for p in range(planes):
-        copy = pltpu.make_async_copy(grid.at[pl.ds(p * levels * lat_pad, levels * lat_pad)], grid_hbm.at[:, pl.ds(p * LANES, LANES)], grid_sem.at[p])
-        copy.start()
-        grid_out.append(copy)
 
     landed = recv_b.at[pl.ds(0, (chunks - 1) * (group - 1) * msg)]
     pltpu.make_async_copy(landed, landed, recv_sem_b).wait()
@@ -202,7 +190,8 @@
             h_hi, h_lo = split(jnp.concatenate([jnp.concatenate(re, axis=0), jnp.concatenate(im, axis=0)], axis=1))
             leg_hi, leg_lo = split(leg[m])
             s_val = dot(leg_hi, h_hi) + dot(leg_lo, h_hi) + dot(leg_hi, h_lo)
-            spec[m] = jnp.transpose(s_val).reshape(2, levels, degs)
+            spec[m, 0] = s_val[:, :levels]
+            spec[m, 1] = s_val[:, levels:]
             return carry
 
         lax.fori_loop(0, per_group, back_body, 0)
@@ -213,8 +202,7 @@
 
     for copy in outs:
         copy.wait()
-    for copy in grid_out:
-        copy.wait()
+    pltpu.make_async_copy(grid, grid_hbm, grid_sem).wait()
     sent = send_a.at[pl.ds(0, (group - 1) * chunks * msg)]
     pltpu.make_async_copy(sent, sent, send_sem_a).wait()
     pltpu.make_async_copy(sent, sent, send_sem_b).wait()
@@ -228,20 +216,19 @@
         waves = wave_loc * group
         lon = 2 * waves
         lat_loc = legendre.shape[2] // group
-        lat_pad = -(-lat_loc // SUB) * SUB
+        coef_t = jnp.transpose(coef, (0, 1, 3, 2))
         inv, fwd = (jnp.asarray(x) for x in fourier_matrices(waves))
-        planes = -(-lon // LANES)
         total = group * lat_loc // QUAD * wave_loc * SUB
-        dims = (group, wave_loc, levels, degs, lat_loc, lat_pad, waves, lon)
+        dims = (group, wave_loc, levels, degs, lat_loc, waves, lon)
         hbm = pl.BlockSpec(memory_space=pl.ANY)
         dma = pltpu.SemaphoreType.DMA
         grid, spec = pl.pallas_call(
             functools.partial(kernel, dims),
-            out_shape=(jax.ShapeDtypeStruct((levels * lat_pad, planes * LANES), F32), jax.ShapeDtypeStruct(coef.shape, F32)),
+            out_shape=(jax.ShapeDtypeStruct((lat_loc, lon, levels), F32), jax.ShapeDtypeStruct(coef_t.shape, F32)),
             in_specs=[hbm, hbm, hbm, hbm, pl.BlockSpec(memory_space=pltpu.SMEM)],
             out_specs=(hbm, hbm),
             scratch_shapes=[
-                pltpu.VMEM(coef.shape, F32),
+                pltpu.VMEM(coef_t.shape, F32),
                 pltpu.VMEM((wave_loc, degs, legendre.shape[2]), F32),
                 pltpu.VMEM(inv.shape, BF16),
                 pltpu.VMEM(fwd.shape, BF16),
@@ -249,13 +236,13 @@
                 pltpu.VMEM((total, levels), F32),
                 pltpu.VMEM((total, levels), F32),
                 pltpu.VMEM((total, levels), F32),
-                pltpu.VMEM((planes * levels * lat_pad, LANES), F32),
-                pltpu.VMEM(coef.shape, F32),
-                dma((2, GROUPS)), dma((2,)), dma, dma((lat_loc // QUAD,)), dma, dma, dma((GROUPS,)), dma((GROUPS,)), dma((planes,)),
+                pltpu.VMEM((lat_loc, lon, levels), F32),
+                pltpu.VMEM(coef_t.shape, F32),
+                dma((2, GROUPS)), dma((2,)), dma, dma((lat_loc // QUAD,)), dma, dma, dma((GROUPS,)), dma((GROUPS,)), dma,
             ],
             compiler_params=pltpu.CompilerParams(collective_id=0, has_side_effects=True, vmem_limit_bytes=56 * 2**20),
             name='transform_pair',
-        )(coef, legendre, inv, fwd, gauss_weight)
-        return grid.reshape(levels, lat_pad, planes * LANES)[:, :lat_loc, :lon], spec
+        )(coef_t, legendre, inv, fwd, gauss_weight)
+        return jnp.transpose(grid, (2, 0, 1)), jnp.transpose(spec, (0, 1, 3, 2))
 
     return jax.shard_map(per_device, mesh=mesh, in_specs=(P('w', None, 'lev', None), P(None, None, None), P(None)), out_specs=(P('lev', 'w', None), P('w', None, 'lev', None)), check_vma=False)

time: 100 us -> 87.3 us (0.87)
  local copies, waits for them, and re-layouts: 16.7 us -> 5.81 us
  Pallas kernels: 82.6 us -> 80.8 us
    unnamed x3 -> x4, local copies, waits for them, and re-layouts: 16.7 us -> 5.81 us
    pallas_call x1, Pallas kernels: 82.6 us -> 80.8 us  [per_device(): pl.pallas_call(functools.partial(kernel, dims), out_shape=(jax.ShapeDtype...]
where the time goes in v1:
time: 87.3 us; the launch traced here: 87.2 us
  Pallas kernels  80.8 us (93%)
  local copies, waits for them, and re-layouts  5.81 us (7%)
    pallas_call x1, Pallas kernels, per_device(): pl.pallas_call(functools.partial(kernel, dims), out_shape=(jax.ShapeDtype...  80.8 us
    unnamed x4, local copies, waits for them, and re-layouts  5.81 us

profile of v1, /device:TPU:113, one launch (start us, length us, event | category | flops | bytes accessed | tf_op | source)
XLA Modules:
  0.0 87.2 jit_solution(16888124097844876774)
XLA Ops:
  0.6 80.8 %transform_pair.1 = (f32[20,320,128]{2,1,0:T(8,128)}, f32[20,2,160,128]{3,2,1,0:T(8,128)}) custom-call(f32[20,2,160,128]{3,2,1,0:T(8,128)} %bitcast.3, f32[160,160,160]{2,1,0:T(8,128)} %leg_hbm.1, bf16[320,960]{1,0:T(8,128)(2,1)} %constant.4.clone.inv_hbm, bf16[320,960]{1,0:T(8,128)(2,1)} %constant.5.clone.fwd_hbm, f32[160]{0:T(256)} %wt_ref.1), custom_call_target="tpu_custom_call" | custom-call | tf_op jit(solution)/shard_map/transform_pair/pallas_call | solution.py:225
  81.4 0.0 copy-start
  81.4 4.1 %copy.9 = f32[128,20,320]{0,2,1:T(8,128)} copy(f32[128,20,320]{0,2,1:T(8,128)} %bitcast.5) | data formatting | bytes 6553600
  85.5 0.0 copy-done
  85.5 1.7 %copy.10 = f32[20,2,128,160]{2,3,1,0:T(8,128)} copy(f32[20,2,128,160]{2,3,1,0:T(8,128)S(1)} %bitcast.4) | data formatting | bytes 6553600
Async XLA Ops:
  81.4 4.1 %copy-start = (f32[20,2,160,128]{3,2,1,0:T(8,128)S(1)}, f32[20,2,160,128]{3,2,1,0:T(8,128)}, u32[]{:S(2)}) copy-start(f32[20,2,160,128]{3,2,1,0:T(8,128)} %get-tuple-element.5) | copy-start | bytes 9830404

commit v2 on v1

--- a/solution.py
+++ b/solution.py
@@ -47,9 +47,9 @@
     return lax.dot_general(a, b, (dims, ((), ())), preferred_element_type=F32)
 
 
-def kernel(dims, coef_hbm, leg_hbm, inv_hbm, fwd_hbm, wt_ref, grid_hbm, spec_hbm,
-           coef, leg, inv, fwd, send_a, recv_a, send_b, recv_b, grid, spec,
-           load_sem, mat_sem, send_sem_a, recv_sem_a, send_sem_b, recv_sem_b, last_sem, out_sem, grid_sem):
+def kernel(dims, coef_hbm, leg_hbm, inv_hbm, fwd_hbm, wt_ref, grid, spec,
+           coef, leg, inv, fwd, send_a, recv_a, send_b, recv_b,
+           load_sem, mat_sem, send_sem_a, recv_sem_a, send_sem_b, recv_sem_b, last_sem):
     group, wave_loc, levels, degs, lat_loc, waves, lon = dims
     chunks = lat_loc // QUAD
     per_group = wave_loc // GROUPS
@@ -165,13 +165,10 @@
                 for off in order:
                     copy_b(off, c, g * part, part, last_sem.at[g]).start()
 
-        lats = pl.ds(c * QUAD, QUAD)
-        pltpu.make_async_copy(grid.at[lats], grid_hbm.at[lats], grid_sem).start()
         recv_b[rows((c * group + me) * msg, msg), :] = send_b[rows((c * group + me) * msg, msg), :]
 
     landed = recv_b.at[pl.ds(0, (chunks - 1) * (group - 1) * msg)]
     pltpu.make_async_copy(landed, landed, recv_sem_b).wait()
-    outs = []
     for g in range(GROUPS):
         landed = recv_b.at[pl.ds(0, (group - 1) * part)]
         pltpu.make_async_copy(landed, landed, last_sem.at[g]).wait()
@@ -195,14 +192,7 @@
             return carry
 
         lax.fori_loop(0, per_group, back_body, 0)
-        own = pl.ds(g * per_group, per_group)
-        copy = pltpu.make_async_copy(spec.at[own], spec_hbm.at[own], out_sem.at[g])
-        copy.start()
-        outs.append(copy)
-
-    for copy in outs:
-        copy.wait()
-    pltpu.make_async_copy(grid, grid_hbm, grid_sem).wait()
+
     sent = send_a.at[pl.ds(0, (group - 1) * chunks * msg)]
     pltpu.make_async_copy(sent, sent, send_sem_a).wait()
     pltpu.make_async_copy(sent, sent, send_sem_b).wait()
@@ -221,12 +211,13 @@
         total = group * lat_loc // QUAD * wave_loc * SUB
         dims = (group, wave_loc, levels, degs, lat_loc, waves, lon)
         hbm = pl.BlockSpec(memory_space=pl.ANY)
+        vmem = pl.BlockSpec(memory_space=pltpu.VMEM)
         dma = pltpu.SemaphoreType.DMA
         grid, spec = pl.pallas_call(
             functools.partial(kernel, dims),
-            out_shape=(jax.ShapeDtypeStruct((lat_loc, lon, levels), F32), jax.ShapeDtypeStruct(coef_t.shape, F32)),
+            out_shape=(pltpu.VMEM((lat_loc, lon, levels), F32), pltpu.VMEM(coef_t.shape, F32)),
             in_specs=[hbm, hbm, hbm, hbm, pl.BlockSpec(memory_space=pltpu.SMEM)],
-            out_specs=(hbm, hbm),
+            out_specs=(vmem, vmem),
             scratch_shapes=[
                 pltpu.VMEM(coef_t.shape, F32),
                 pltpu.VMEM((wave_loc, degs, legendre.shape[2]), F32),
@@ -236,11 +227,9 @@
                 pltpu.VMEM((total, levels), F32),
                 pltpu.VMEM((total, levels), F32),
                 pltpu.VMEM((total, levels), F32),
-                pltpu.VMEM((lat_loc, lon, levels), F32),
-                pltpu.VMEM(coef_t.shape, F32),
-                dma((2, GROUPS)), dma((2,)), dma, dma((lat_loc // QUAD,)), dma, dma, dma((GROUPS,)), dma((GROUPS,)), dma,
+                dma((2, GROUPS)), dma((2,)), dma, dma((lat_loc // QUAD,)), dma, dma, dma((GROUPS,)),
             ],
-            compiler_params=pltpu.CompilerParams(collective_id=0, has_side_effects=True, vmem_limit_bytes=56 * 2**20),
+            compiler_params=pltpu.CompilerParams(collective_id=0, has_side_effects=True, vmem_limit_bytes=48 * 2**20),
             name='transform_pair',
         )(coef_t, legendre, inv, fwd, gauss_weight)
         return jnp.transpose(grid, (2, 0, 1)), jnp.transpose(spec, (0, 1, 3, 2))

time: 87.3 us -> 84 us (0.962)
  local copies, waits for them, and re-layouts: 5.81 us -> 3.42 us
  Pallas kernels: 80.8 us -> 79.8 us
    unnamed x4 -> x2, local copies, waits for them, and re-layouts: 5.81 us -> 3.42 us
    pallas_call x1, Pallas kernels: 80.8 us -> 79.8 us  [per_device(): pl.pallas_call(functools.partial(kernel, dims), out_shape=(pltpu.VMEM((la...]
where the time goes in v2:
time: 84 us; the launch traced here: 83.9 us
  Pallas kernels  79.8 us (95%)
  local copies, waits for them, and re-layouts  3.42 us (4%)
    pallas_call x1, Pallas kernels, per_device(): pl.pallas_call(functools.partial(kernel, dims), out_shape=(pltpu.VMEM((la...  79.8 us
    unnamed x2, local copies, waits for them, and re-layouts  3.42 us

profile of v2, /device:TPU:113, one launch (start us, length us, event | category | flops | bytes accessed | tf_op | source)
XLA Modules:
  0.0 83.9 jit_solution(18292684266835080053)
XLA Ops:
  0.6 79.8 %transform_pair.1 = (f32[20,320,128]{2,1,0:T(8,128)S(1)}, f32[20,2,160,128]{3,2,1,0:T(8,128)S(1)}) custom-call(f32[20,2,160,128]{3,2,1,0:T(8,128)} %bitcast.5, f32[160,160,160]{2,1,0:T(8,128)} %leg_hbm.1, bf16[320,960]{1,0:T(8,128)(2,1)} %constant.4.clone.inv_hbm, bf16[320,960]{1,0:T(8,128)(2,1)} %constant.5.clone.fwd_hbm, f32[160]{0:T(256)} %wt_ref.1), custom_call_target="tpu_custom_call" | custom-call | tf_op jit(solution)/shard_map/transform_pair/pallas_call | solution.py:216
  80.5 1.7 %copy.9 = f32[128,20,320]{0,2,1:T(8,128)} copy(f32[128,20,320]{0,2,1:T(8,128)S(1)} %bitcast.4) | data formatting | bytes 6553600
  82.2 1.7 %copy.10 = f32[20,2,128,160]{2,3,1,0:T(8,128)} copy(f32[20,2,128,160]{2,3,1,0:T(8,128)S(1)} %bitcast.3) | data formatting | bytes 6553600

commit v3 on v2

v3 whole, which is shorter than its diff:
```python
import functools

import jax
import jax.numpy as jnp
import ml_dtypes
import numpy as np
from jax import lax
from jax.experimental import pallas as pl
from jax.experimental.pallas import tpu as pltpu
from jax.sharding import PartitionSpec as P

MESH = pl.DeviceIdType.MESH
F32, BF16 = jnp.float32, jnp.bfloat16
SUB = 8
QUAD = 4
SIZES_A = (2, 4, 6, 8)
SIZES_B = (8, 6, 4, 2)
CORES = 2
BLOCK = 4
OWN = 32
RELAYED = 2


def split_np(mat):
    hi = mat.astype(np.float32).astype(ml_dtypes.bfloat16)
    lo = (mat - hi.astype(np.float64)).astype(np.float32).astype(ml_dtypes.bfloat16)
    return hi, lo


def fourier_matrices(waves):
    lon = 2 * waves
    m = np.arange(waves)[:, None]
    n = np.arange(lon)[None, :]
    ang = 2.0 * np.pi * ((m * n) % lon) / lon
    fwd = np.concatenate([np.cos(ang), -np.sin(ang)], axis=0)
    scale = np.where(np.arange(waves) == 0, 1.0, 2.0) / lon
    inv = (fwd * np.tile(scale, 2)[:, None]).T
    out = []
    for mat in (inv, fwd):
        hi, lo = split_np(mat)
        out.append(np.concatenate([hi, hi, lo], axis=1))
    return out


def split(x):
    hi = x.astype(BF16)
    lo = (x - hi.astype(F32)).astype(BF16)
    return hi, lo


def dot(a, b, dims=((1,), (0,))):
    return lax.dot_general(a, b, (dims, ((), ())), preferred_element_type=F32)


def kernel(dims, coef_hbm, leg_hbm, inv_hbm, fwd_hbm, wt_ref, grid, spec,
           coef, leg, inv, fwd, send_a, recv_a, send_b, recv_b,
           tri, leg_tri, spread, leg_own, leg_own_t, part_own, part_mate, part_in, relay,
           load_sem, mat_sem, send_sem_a, recv_sem_a, send_sem_b, recv_sem_b, last_sem,
           tri_load, tri_send, tri_recv, mate_send, mate_recv, part_send, part_recv, relay_send, relay_recv):
    group, wave_loc, levels, degs, lat_loc, waves, lon = dims
    chunks = lat_loc // QUAD
    msg = wave_loc * SUB
    chips = group // CORES
    tri_num = CORES * wave_loc
    tri_m = waves - tri_num
    tri_deg = degs - tri_m
    full = group - CORES
    blocks = wave_loc // BLOCK
    me = lax.axis_index('w')
    core = lax.rem(me, CORES)
    chip = lax.div(me, CORES)
    mate = me + 1 - 2 * core
    is_full = me < full
    is_tri = me >= full

    def starts(sizes):
        return [(g, sum(sizes[:g]), size) for g, size in enumerate(sizes)]

    def rows(start, size):
        return pl.ds(pl.multiple_of(start, SUB), size)

    def skip(b):
        return BLOCK * b // SUB * SUB

    for m in range(tri_num):
        gap = skip(m // BLOCK)
        if gap:
            for r in range(2):
                tri[m, r, 0:gap, :] = jnp.zeros((gap, levels), F32)

    barrier = pltpu.get_barrier_semaphore()
    for off in range(1, group):
        pl.semaphore_signal(barrier, inc=1, device_id={'w': lax.rem(me + off, group)}, device_id_type=MESH)

    def load_pair(g, start, size):
        own = pl.ds(start, size)
        return (pltpu.make_async_copy(coef_hbm.at[own], coef.at[own], load_sem.at[0, g]),
                pltpu.make_async_copy(leg_hbm.at[pl.ds(me * wave_loc + start, size)], leg.at[own], load_sem.at[1, g]))

    def load_block(b):
        gap = skip(b)
        return pltpu.make_async_copy(
            coef_hbm.at[pl.ds(BLOCK * (b % blocks), BLOCK), :, pl.ds(tri_m + gap, tri_deg - gap), :],
            tri.at[pl.ds(BLOCK * b, BLOCK), :, pl.ds(gap, tri_deg - gap), :], tri_load.at[b])

    @pl.when(is_full)
    def _():
        for args in starts(SIZES_A):
            for copy in load_pair(*args):
                copy.start()

    for b in range(CORES * blocks):
        @pl.when(me == full + b // blocks)
        def _():
            load_block(b).start()

    leg_tri_copy = pltpu.make_async_copy(leg_hbm.at[pl.ds(tri_m, tri_num), pl.ds(tri_m, tri_deg), :], leg_tri, mat_sem.at[2])
    mats = [leg_tri_copy, pltpu.make_async_copy(inv_hbm, inv, mat_sem.at[0]), pltpu.make_async_copy(fwd_hbm, fwd, mat_sem.at[1])]
    for copy in mats:
        copy.start()

    low = lax.broadcasted_iota(jnp.int32, (SUB, levels), 0) < QUAD

    def copy_a(off, c, start, size):
        dst = lax.rem(me + off, group)
        return pltpu.make_async_remote_copy(
            src_ref=send_a.at[rows((dst * chunks + c) * msg + start, size)],
            dst_ref=recv_a.at[rows((c * group + me) * msg + start, size)],
            send_sem=send_sem_a, recv_sem=recv_sem_a.at[c], device_id={'w': dst}, device_id_type=MESH)

    def copy_b(dst, c, start, size, sem):
        return pltpu.make_async_remote_copy(
            src_ref=send_b.at[rows((c * group + dst) * msg + start, size)],
            dst_ref=recv_b.at[rows((c * group + me) * msg + start, size)],
            send_sem=send_sem_b, recv_sem=sem, device_id={'w': dst}, device_id_type=MESH)

    def copy_relay(dst, c):
        slot = c * CORES + lax.rem(dst, CORES)
        return pltpu.make_async_remote_copy(
            src_ref=send_b.at[rows((c * group + dst) * msg, msg)], dst_ref=relay.at[rows(slot * msg, msg)],
            send_sem=send_sem_b, recv_sem=relay_recv.at[slot], device_id={'w': full + core}, device_id_type=MESH)

    def copy_onward(c, e):
        slot = c * CORES + e
        return pltpu.make_async_remote_copy(
            src_ref=relay.at[rows(slot * msg, msg)], dst_ref=recv_b.at[rows((c * group + core) * msg, msg)],
            send_sem=relay_send, recv_sem=recv_sem_b, device_id={'w': group // 2 + e}, device_id_type=MESH)

    def copy_tri(b, lane, dst):
        gap = skip(b)
        ref = tri.at[pl.ds(BLOCK * b, BLOCK), :, pl.ds(gap, tri_deg - gap), :]
        return pltpu.make_async_remote_copy(
            src_ref=ref, dst_ref=ref, send_sem=tri_send.at[lane, b % blocks], recv_sem=tri_recv.at[b],
            device_id={'w': dst}, device_id_type=MESH)

    def copy_mate(b):
        gap = skip(b)
        return pltpu.make_async_remote_copy(
            src_ref=part_own.at[pl.ds(BLOCK * b, BLOCK), :, pl.ds(gap, tri_deg - gap), :],
            dst_ref=part_mate.at[pl.ds(BLOCK * (b % blocks), BLOCK), :, pl.ds(gap, tri_deg - gap), :],
            send_sem=mate_send.at[b], recv_sem=mate_recv.at[b], device_id={'w': mate}, device_id_type=MESH)

    def copy_part(b):
        gap = skip(b)
        return pltpu.make_async_remote_copy(
            src_ref=part_own.at[pl.ds(BLOCK * b, BLOCK), :, pl.ds(gap, tri_deg - gap), :],
            dst_ref=part_in.at[chip, pl.ds(BLOCK * (b % blocks), BLOCK), :, pl.ds(gap, tri_deg - gap), :],
            send_sem=part_send.at[b], recv_sem=part_recv.at[chip, b], device_id={'w': full + core}, device_id_type=MESH)

    def wait_rows(ref, sem, count):
        landed = ref.at[pl.ds(0, count)]
        pltpu.make_async_copy(landed, landed, sem).wait()

    order = [group // 2, 2, group - 2, group // 2 + 1, 3, group - 1, 1]
    order = order if sorted(order) == list(range(1, group)) else list(range(1, group))

    @pl.when(is_full)
    def _():
        for g, start, size in starts(SIZES_A):
            for copy in load_pair(g, start, size):
                copy.wait()

            def legendre_body(i, carry):
                m = start + i
                leg_hi, leg_lo = split(jnp.transpose(leg[m]))
                c_hi, c_lo = split(jnp.concatenate([coef[m, 0], coef[m, 1]], axis=1))
                f = dot(leg_hi, c_hi) + dot(leg_lo, c_hi) + dot(leg_hi, c_lo)
                for t in range(group * lat_loc // SUB):
                    re = f[t * SUB:(t + 1) * SUB, :levels]
                    im = f[t * SUB:(t + 1) * SUB, levels:]
                    send_a[rows((2 * t * wave_loc + m) * SUB, SUB), :] = jnp.where(low, re, pltpu.roll(im, QUAD, 0))
                    send_a[rows(((2 * t + 1) * wave_loc + m) * SUB, SUB), :] = jnp.where(low, pltpu.roll(re, QUAD, 0), im)
                return carry

            lax.fori_loop(0, size, legendre_body, 0)
            if g == 0:
                pl.semaphore_wait(barrier, group - 1)
            for off in order:
                copy_a(off, 0, start * SUB, size * SUB).start()

        @pl.loop(1, chunks)
        def _(c):
            for off in order:
                copy_a(off, c, 0, msg).start()

        @pl.loop(0, chunks)
        def _(c):
            recv_a[rows((c * group + me) * msg, msg), :] = send_a[rows((me * chunks + c) * msg, msg), :]

    @pl.when(is_tri)
    def _():
        pl.semaphore_wait(barrier, group - 1)
        for b in range(CORES * blocks):
            @pl.when(core == b // blocks)
            def _():
                load_block(b).wait()
                for lane, dst in enumerate([CORES + core, core, 2 * CORES + core, mate]):
                    copy_tri(b, lane, dst).start()

    leg_tri_copy.wait()
    lat_all = group * lat_loc

    def spread_body(m, carry):
        x = jnp.concatenate([leg_tri[m], jnp.zeros((levels - tri_deg, lat_all), F32)], axis=0)
        eighth, lane = m // SUB, lax.rem(m, SUB)
        spread[pl.ds(eighth * lat_all * SUB + lane, lat_all, stride=SUB), :] = jnp.transpose(x)
        return carry

    lax.fori_loop(0, tri_num, spread_body, 0)

    def own_body(m, carry):
        eighth, lane = m // SUB, lax.rem(m, SUB)
        own = spread[pl.ds((eighth * lat_all + me * lat_loc) * SUB + lane, OWN, stride=SUB), :]
        own = jnp.where(lax.broadcasted_iota(jnp.int32, (OWN, levels), 0) < lat_loc, own, 0.0)
        leg_own[m] = own
        leg_own_t[m] = jnp.transpose(own)[:tri_deg]
        return carry

    lax.fori_loop(0, tri_num, own_body, 0)

    for b in range(CORES * blocks):
        @pl.when(jnp.logical_and(is_full, core == b // blocks))
        def _():
            copy_tri(b, 3, mate).wait_recv()
            copy_tri(b, 3, mate).start()
    for b in range(CORES * blocks):
        @pl.when(core != b // blocks)
        def _():
            copy_tri(b, 3, mate).wait_recv()

    def tri_body(m, carry):
        own_hi, own_lo = split(leg_own[m][:, :tri_deg])
        c_hi, c_lo = split(jnp.concatenate([tri[m, 0], tri[m, 1]], axis=1))
        f = dot(own_hi, c_hi) + dot(own_lo, c_hi) + dot(own_hi, c_lo)
        for c in range(chunks):
            t = c // 2
            re = f[t * SUB:(t + 1) * SUB, :levels]
            im = f[t * SUB:(t + 1) * SUB, levels:]
            tile = jnp.where(low, pltpu.roll(re, QUAD, 0), im) if c % 2 else jnp.where(low, re, pltpu.roll(im, QUAD, 0))
            recv_a[rows(((c * group + full) * wave_loc + m) * SUB, SUB), :] = tile
        return carry

    lax.fori_loop(0, tri_num, tri_body, 0)

    for copy in mats[1:]:
        copy.wait()

    @pl.loop(0, chunks)
    def _(c):
        @pl.when(is_full)
        def _():
            wait_rows(recv_a, recv_sem_a.at[c], (full - 1) * msg)

        @pl.when(is_tri)
        def _():
            wait_rows(recv_a, recv_sem_a.at[c], full * msg)

        @pl.loop(0, QUAD // 2)
        def _(pair):
            halves = []
            for u in range(2):
                row = c * (group * msg) + 2 * pair + u
                re = recv_a[pl.ds(row, waves, stride=SUB), :]
                im = recv_a[pl.ds(row + QUAD, waves, stride=SUB), :]
                halves.append(jnp.concatenate([re, im], axis=0))
            f_hi, f_lo = split(jnp.concatenate(halves, axis=1))
            g_val = dot(inv[...], jnp.concatenate([f_hi, f_lo, f_hi], axis=0))
            for u in range(2):
                grid[c * QUAD + 2 * pair + u] = g_val[:, u * levels:(u + 1) * levels]
            q_hi, q_lo = split(g_val * g_val)
            h = dot(fwd[...], jnp.concatenate([q_hi, q_lo, q_hi], axis=0))
            for u in range(2):
                row = c * (group * msg) + 2 * pair + u
                hw = h[:, u * levels:(u + 1) * levels] * wt_ref[me * lat_loc + c * QUAD + 2 * pair + u]
                send_b[pl.ds(row, waves, stride=SUB), :] = hw[:waves]
                send_b[pl.ds(row + QUAD, waves, stride=SUB), :] = hw[waves:]

        @pl.when(c < chunks - 1)
        def _():
            for off in order:
                dst = lax.rem(me + off, group)
                by_relay = jnp.logical_and(jnp.logical_and(chip == 0, dst >= group // 2), c < RELAYED)

                @pl.when(jnp.logical_and(dst < full, by_relay))
                def _():
                    copy_relay(dst, c).start()

                @pl.when(jnp.logical_and(dst < full, jnp.logical_not(by_relay)))
                def _():
                    copy_b(dst, c, 0, msg, recv_sem_b).start()

        @pl.when(c == chunks - 1)
        def _():
            for g, start, size in starts(SIZES_B):
                for off in order:
                    dst = lax.rem(me + off, group)

                    @pl.when(dst < full)
                    def _():
                        copy_b(dst, c, start * SUB, size * SUB, last_sem.at[g]).start()

        @pl.when(is_full)
        def _():
            recv_b[rows((c * group + me) * msg, msg), :] = send_b[rows((c * group + me) * msg, msg), :]

    zero = jnp.zeros((SUB, levels), F32)

    def part_body(i, carry):
        m = lax.rem(i + (1 - core) * wave_loc, tri_num)
        re, im = [], []
        for t in range(OWN // SUB):
            a, b = (send_b[rows((c * waves + tri_m + m) * SUB, SUB), :] if c < chunks else zero for c in (2 * t, 2 * t + 1))
            re.append(jnp.where(low, a, pltpu.roll(b, QUAD, 0)))
            im.append(jnp.where(low, pltpu.roll(a, QUAD, 0), b))
        h_hi, h_lo = split(jnp.concatenate([jnp.concatenate(re, axis=0), jnp.concatenate(im, axis=0)], axis=1))
        own_hi, own_lo = split(leg_own_t[m])
        p_val = dot(own_hi, h_hi) + dot(own_lo, h_hi) + dot(own_hi, h_lo)
        part_own[m, 0] = p_val[:, :levels]
        part_own[m, 1] = p_val[:, levels:]
        return carry

    lax.fori_loop(0, wave_loc, part_body, 0)
    for b in range(CORES * blocks):
        @pl.when(core != b // blocks)
        def _():
            copy_mate(b).start()
    lax.fori_loop(wave_loc, tri_num, part_body, 0)
    for b in range(CORES * blocks):
        @pl.when(core == b // blocks)
        def _():
            copy_mate(b).wait_recv()

            @pl.loop(0, BLOCK)
            def _(i):
                gap = skip(b)
                for r in range(2):
                    part_own[BLOCK * b + i, r, gap:, :] += part_mate[BLOCK * (b % blocks) + i, r, gap:, :]

        @pl.when(jnp.logical_and(is_full, core == b // blocks))
        def _():
            copy_part(b).start()

    @pl.when(is_tri)
    def _():
        for c in range(RELAYED):
            for e in range(CORES):
                slot = c * CORES + e
                landed = relay.at[pl.ds(slot * msg, msg)]
                pltpu.make_async_copy(landed, landed, relay_recv.at[slot]).wait()
                copy_onward(c, e).start()

    @pl.when(is_full)
    def _():
        wait_rows(recv_b, recv_sem_b, (chunks - 1) * (group - 1) * msg)
        for g, start, size in starts(SIZES_B):
            wait_rows(recv_b, last_sem.at[g], (group - 1) * size * SUB)

            def back_body(i, carry):
                m = start + i
                re, im = [], []
                for t in range(group * lat_loc // SUB):
                    tiles = []
                    for q in (2 * t, 2 * t + 1):
                        s, c = divmod(q, chunks)
                        tiles.append(recv_b[rows(((c * group + s) * wave_loc + m) * SUB, SUB), :])
                    a, b = tiles
                    re.append(jnp.where(low, a, pltpu.roll(b, QUAD, 0)))
                    im.append(jnp.where(low, pltpu.roll(a, QUAD, 0), b))
                h_hi, h_lo = split(jnp.concatenate([jnp.concatenate(re, axis=0), jnp.concatenate(im, axis=0)], axis=1))
                leg_hi, leg_lo = split(leg[m])
                s_val = dot(leg_hi, h_hi) + dot(leg_lo, h_hi) + dot(leg_hi, h_lo)
                spec[m, 0] = s_val[:, :levels]
                spec[m, 1] = s_val[:, levels:]
                return carry

            lax.fori_loop(0, size, back_body, 0)

    for b in range(CORES * blocks):
        @pl.when(me == full + b // blocks)
        def _():
            gap = skip(b)
            for src in range(chips - 1):
                landed = part_in.at[src, pl.ds(BLOCK * (b % blocks), BLOCK), :, pl.ds(gap, tri_deg - gap), :]
                pltpu.make_async_copy(landed, landed, part_recv.at[src, b]).wait()

            @pl.loop(0, BLOCK)
            def _(i):
                m = BLOCK * (b % blocks) + i
                for r in range(2):
                    acc = part_own[BLOCK * b + i, r, gap:, :]
                    for src in range(chips - 1):
                        acc = acc + part_in[src, m, r, gap:, :]
                    spec[m, r, :tri_m + gap, :] = jnp.zeros((tri_m + gap, levels), F32)
                    spec[m, r, tri_m + gap:, :] = acc

    @pl.when(is_full)
    def _():
        wait_rows(send_a, send_sem_a, (group - 1) * chunks * msg)
        wait_rows(send_b, send_sem_b, (full - 1) * chunks * msg)

    @pl.when(is_tri)
    def _():
        wait_rows(send_b, send_sem_b, full * chunks * msg)
        wait_rows(relay, relay_send, RELAYED * CORES * msg)

    for b in range(CORES * blocks):
        @pl.when(core == b // blocks)
        def _():
            copy_tri(b, 3, mate).wait_send()

        @pl.when(core != b // blocks)
        def _():
            copy_mate(b).wait_send()

        @pl.when(me == full + b // blocks)
        def _():
            for lane in range(3):
                copy_tri(b, lane, mate).wait_send()

        @pl.when(jnp.logical_and(is_full, core == b // blocks))
        def _():
            copy_part(b).wait_send()


def solution(mesh):
    group = mesh.shape['w']

    def per_device(coef, legendre, gauss_weight):
        wave_loc, _, levels, degs = coef.shape
        waves = wave_loc * group
        lon = 2 * waves
        lat_loc = legendre.shape[2] // group
        coef_t = jnp.transpose(coef, (0, 1, 3, 2))
        inv, fwd = (jnp.asarray(x) for x in fourier_matrices(waves))
        tri_num = CORES * wave_loc
        tri_deg = degs - waves + tri_num
        blocks = tri_num // BLOCK
        total = group * lat_loc // QUAD * wave_loc * SUB
        dims = (group, wave_loc, levels, degs, lat_loc, waves, lon)
        hbm = pl.BlockSpec(memory_space=pl.ANY)
        vmem = pl.BlockSpec(memory_space=pltpu.VMEM)
        dma = pltpu.SemaphoreType.DMA
        grid, spec = pl.pallas_call(
            functools.partial(kernel, dims),
            out_shape=(pltpu.VMEM((lat_loc, lon, levels), F32), pltpu.VMEM(coef_t.shape, F32)),
            in_specs=[hbm, hbm, hbm, hbm, pl.BlockSpec(memory_space=pltpu.SMEM)],
            out_specs=(vmem, vmem),
            scratch_shapes=[
                pltpu.VMEM(coef_t.shape, F32),
                pltpu.VMEM((wave_loc, degs, legendre.shape[2]), F32),
                pltpu.VMEM(inv.shape, BF16),
                pltpu.VMEM(fwd.shape, BF16),
                pltpu.VMEM((total, levels), F32),
                pltpu.VMEM((total, levels), F32),
                pltpu.VMEM((total, levels), F32),
                pltpu.VMEM((total, levels), F32),
                pltpu.VMEM((tri_num, 2, tri_deg, levels), F32),
                pltpu.VMEM((tri_num, tri_deg, legendre.shape[2]), F32),
                pltpu.VMEM((tri_num * legendre.shape[2] + OWN * SUB, levels), F32),
                pltpu.VMEM((tri_num, OWN, levels), F32),
                pltpu.VMEM((tri_num, tri_deg, OWN), F32),
                pltpu.VMEM((tri_num, 2, tri_deg, levels), F32),
                pltpu.VMEM((wave_loc, 2, tri_deg, levels), F32),
                pltpu.VMEM((group // CORES - 1, wave_loc, 2, tri_deg, levels), F32),
                pltpu.VMEM((RELAYED * CORES * wave_loc * SUB, levels), F32),
                dma((2, len(SIZES_A))), dma((3,)), dma, dma((lat_loc // QUAD,)), dma, dma, dma((len(SIZES_B),)),
                dma((blocks,)), dma((4, blocks // CORES)), dma((blocks,)), dma((blocks,)), dma((blocks,)),
                dma((blocks,)), dma((group // CORES - 1, blocks)), dma, dma((RELAYED * CORES,)),
            ],
            compiler_params=pltpu.CompilerParams(collective_id=0, has_side_effects=True, vmem_limit_bytes=48 * 2**20),
            name='transform_pair',
        )(coef_t, legendre, inv, fwd, gauss_weight)
        return jnp.transpose(grid, (2, 0, 1)), jnp.transpose(spec, (0, 1, 3, 2))

    return jax.shard_map(per_device, mesh=mesh, in_specs=(P('w', None, 'lev', None), P(None, None, None), P(None)), out_specs=(P('lev', 'w', None), P('w', None, 'lev', None)), check_vma=False)
```

time: 84 us -> 82.4 us (0.981)
  the two profiles are of different devices: /device:TPU:113 before, /device:TPU:112 now
where the time goes in v3:
time: 82.4 us; the launch traced here: 82.3 us
  Pallas kernels  78.2 us (95%)
  local copies, waits for them, and re-layouts  3.42 us (4%)
    pallas_call x1, Pallas kernels, per_device(): pl.pallas_call(functools.partial(kernel, dims), out_shape=(pltpu.VMEM((la...  78.2 us
    unnamed x2, local copies, waits for them, and re-layouts  3.42 us

profile of v3, /device:TPU:112, one launch (start us, length us, event | category | flops | bytes accessed | tf_op | source)
XLA Modules:
  0.0 82.3 jit_solution(6300920044117661244)
XLA Ops:
  0.6 78.2 %transform_pair.1 = (f32[20,320,128]{2,1,0:T(8,128)S(1)}, f32[20,2,160,128]{3,2,1,0:T(8,128)S(1)}) custom-call(f32[20,2,160,128]{3,2,1,0:T(8,128)} %bitcast.5, f32[160,160,160]{2,1,0:T(8,128)} %leg_hbm.1, bf16[320,960]{1,0:T(8,128)(2,1)} %constant.4.clone.inv_hbm, bf16[320,960]{1,0:T(8,128)(2,1)} %constant.5.clone.fwd_hbm, f32[160]{0:T(256)} %wt_ref.1), custom_call_target="tpu_custom_call" | custom-call | tf_op jit(solution)/shard_map/transform_pair/pallas_call | solution.py:463
  78.8 1.7 %copy.9 = f32[128,20,320]{0,2,1:T(8,128)} copy(f32[128,20,320]{0,2,1:T(8,128)S(1)} %bitcast.4) | data formatting | bytes 6553600
  80.6 1.7 %copy.10 = f32[20,2,128,160]{2,3,1,0:T(8,128)} copy(f32[20,2,128,160]{2,3,1,0:T(8,128)S(1)} %bitcast.3) | data formatting | bytes 6553600

commit v4 on v3

--- a/solution.py
+++ b/solution.py
@@ -13,11 +13,14 @@
 F32, BF16 = jnp.float32, jnp.bfloat16
 SUB = 8
 QUAD = 4
-SIZES_A = (2, 4, 6, 8)
+SIZES_A = (4, 4, 4, 8)
+EARLY = 2
 SIZES_B = (8, 6, 4, 2)
 CORES = 2
 BLOCK = 4
 OWN = 32
+HELD = 2
+LAG = 2
 RELAYED = 2
 
 
@@ -54,7 +57,7 @@
 
 def kernel(dims, coef_hbm, leg_hbm, inv_hbm, fwd_hbm, wt_ref, grid, spec,
            coef, leg, inv, fwd, send_a, recv_a, send_b, recv_b,
-           tri, leg_tri, spread, leg_own, leg_own_t, part_own, part_mate, part_in, relay,
+           tri, leg_tri, leg_own, leg_own_t, part_own, part_mate, part_in, relay,
            load_sem, mat_sem, send_sem_a, recv_sem_a, send_sem_b, recv_sem_b, last_sem,
            tri_load, tri_send, tri_recv, mate_send, mate_recv, part_send, part_recv, relay_send, relay_recv):
     group, wave_loc, levels, degs, lat_loc, waves, lon = dims
@@ -72,6 +75,7 @@
     mate = me + 1 - 2 * core
     is_full = me < full
     is_tri = me >= full
+    forwards = chip == chips - 2
 
     def starts(sizes):
         return [(g, sum(sizes[:g]), size) for g, size in enumerate(sizes)]
@@ -134,6 +138,9 @@
             dst_ref=recv_b.at[rows((c * group + me) * msg + start, size)],
             send_sem=send_sem_b, recv_sem=sem, device_id={'w': dst}, device_id_type=MESH)
 
+    def after_parts(dst, c):
+        return jnp.logical_and(jnp.logical_and(chip == 1, dst < CORES), c >= HELD)
+
     def copy_relay(dst, c):
         slot = c * CORES + lax.rem(dst, CORES)
         return pltpu.make_async_remote_copy(
@@ -144,28 +151,48 @@
         slot = c * CORES + e
         return pltpu.make_async_remote_copy(
             src_ref=relay.at[rows(slot * msg, msg)], dst_ref=recv_b.at[rows((c * group + core) * msg, msg)],
-            send_sem=relay_send, recv_sem=recv_sem_b, device_id={'w': group // 2 + e}, device_id_type=MESH)
+            send_sem=relay_send, recv_sem=recv_sem_b.at[c], device_id={'w': group // 2 + e}, device_id_type=MESH)
 
     def copy_tri(b, lane, dst):
         gap = skip(b)
         ref = tri.at[pl.ds(BLOCK * b, BLOCK), :, pl.ds(gap, tri_deg - gap), :]
         return pltpu.make_async_remote_copy(
-            src_ref=ref, dst_ref=ref, send_sem=tri_send.at[lane, b % blocks], recv_sem=tri_recv.at[b],
+            src_ref=ref, dst_ref=ref, send_sem=tri_send.at[lane, b], recv_sem=tri_recv.at[b],
             device_id={'w': dst}, device_id_type=MESH)
+
+    def entry(b, at):
+        return (b // CORES if at == 1 else b) % CORES
+
+    def gets(b):
+        return jnp.where(chip == 1, entry(b, 1), entry(b, 0)) == core
+
+    def keeps(b):
+        return jnp.where(is_tri, b // blocks, b % CORES) == core
+
+    def mate_slot(b):
+        return jnp.where(is_tri, b % blocks, b // CORES)
 
     def copy_mate(b):
         gap = skip(b)
         return pltpu.make_async_remote_copy(
             src_ref=part_own.at[pl.ds(BLOCK * b, BLOCK), :, pl.ds(gap, tri_deg - gap), :],
-            dst_ref=part_mate.at[pl.ds(BLOCK * (b % blocks), BLOCK), :, pl.ds(gap, tri_deg - gap), :],
+            dst_ref=part_mate.at[pl.ds(BLOCK * mate_slot(b), BLOCK), :, pl.ds(gap, tri_deg - gap), :],
             send_sem=mate_send.at[b], recv_sem=mate_recv.at[b], device_id={'w': mate}, device_id_type=MESH)
 
     def copy_part(b):
         gap = skip(b)
+        to_first = chip == 1
+        slot = jnp.where(chip == chips - 2, 1, 0)
+        dst = jnp.where(to_first, core, full + b // blocks)
         return pltpu.make_async_remote_copy(
             src_ref=part_own.at[pl.ds(BLOCK * b, BLOCK), :, pl.ds(gap, tri_deg - gap), :],
-            dst_ref=part_in.at[chip, pl.ds(BLOCK * (b % blocks), BLOCK), :, pl.ds(gap, tri_deg - gap), :],
-            send_sem=part_send.at[b], recv_sem=part_recv.at[chip, b], device_id={'w': full + core}, device_id_type=MESH)
+            dst_ref=part_in.at[slot, pl.ds(BLOCK * (b % blocks), BLOCK), :, pl.ds(gap, tri_deg - gap), :],
+            send_sem=part_send.at[b], recv_sem=part_recv.at[slot, b], device_id={'w': dst}, device_id_type=MESH)
+
+    def wait_part(b, slot):
+        gap = skip(b)
+        landed = part_in.at[slot, pl.ds(BLOCK * (b % blocks), BLOCK), :, pl.ds(gap, tri_deg - gap), :]
+        pltpu.make_async_copy(landed, landed, part_recv.at[slot, b]).wait()
 
     def wait_rows(ref, sem, count):
         landed = ref.at[pl.ds(0, count)]
@@ -173,6 +200,10 @@
 
     order = [group // 2, 2, group - 2, group // 2 + 1, 3, group - 1, 1]
     order = order if sorted(order) == list(range(1, group)) else list(range(1, group))
+
+    def held(off, c):
+        dst_chip = lax.div(lax.rem(me + off, group), CORES)
+        return jnp.logical_and(forwards, jnp.logical_or(dst_chip == 0, jnp.logical_and(dst_chip == 1, c >= HELD)))
 
     @pl.when(is_full)
     def _():
@@ -192,16 +223,29 @@
                     send_a[rows(((2 * t + 1) * wave_loc + m) * SUB, SUB), :] = jnp.where(low, pltpu.roll(re, QUAD, 0), im)
                 return carry
 
-            lax.fori_loop(0, size, legendre_body, 0)
+            lax.fori_loop(0, size, legendre_body, 0, unroll=4)
             if g == 0:
                 pl.semaphore_wait(barrier, group - 1)
             for off in order:
                 copy_a(off, 0, start * SUB, size * SUB).start()
-
-        @pl.loop(1, chunks)
+            if g < EARLY:
+                for off in order:
+                    @pl.when(jnp.logical_not(held(off, 1)))
+                    def _():
+                        copy_a(off, 1, start * SUB, size * SUB).start()
+
+        rest = sum(SIZES_A[:EARLY])
+        for off in order:
+            @pl.when(jnp.logical_not(held(off, 1)))
+            def _():
+                copy_a(off, 1, rest * SUB, (wave_loc - rest) * SUB).start()
+
+        @pl.loop(2, chunks)
         def _(c):
             for off in order:
-                copy_a(off, c, 0, msg).start()
+                @pl.when(jnp.logical_not(held(off, c)))
+                def _():
+                    copy_a(off, c, 0, msg).start()
 
         @pl.loop(0, chunks)
         def _(c):
@@ -214,42 +258,54 @@
             @pl.when(core == b // blocks)
             def _():
                 load_block(b).wait()
-                for lane, dst in enumerate([CORES + core, core, 2 * CORES + core, mate]):
+                for lane, dst in enumerate([full - CORES + entry(b, chips - 2), entry(b, 0), mate]):
                     copy_tri(b, lane, dst).start()
+
+    @pl.when(forwards)
+    def _():
+        for b in range(CORES * blocks):
+            @pl.when(gets(b))
+            def _():
+                copy_tri(b, 2, mate).wait_recv()
+                copy_tri(b, 0, full - 2 * CORES + entry(b, 1)).start()
+                copy_tri(b, 2, mate).start()
+
+        @pl.loop(1, chunks)
+        def _(c):
+            for off in order:
+                @pl.when(held(off, c))
+                def _():
+                    copy_a(off, c, 0, msg).start()
 
     leg_tri_copy.wait()
     lat_all = group * lat_loc
 
-    def spread_body(m, carry):
-        x = jnp.concatenate([leg_tri[m], jnp.zeros((levels - tri_deg, lat_all), F32)], axis=0)
-        eighth, lane = m // SUB, lax.rem(m, SUB)
-        spread[pl.ds(eighth * lat_all * SUB + lane, lat_all, stride=SUB), :] = jnp.transpose(x)
+    pick = lax.broadcasted_iota(jnp.int32, (lat_all, OWN), 0) == lax.broadcasted_iota(jnp.int32, (lat_all, OWN), 1) + me * lat_loc
+    pick = jnp.logical_and(pick, lax.broadcasted_iota(jnp.int32, (lat_all, OWN), 1) < lat_loc)
+    pick = jnp.where(pick, 1.0, 0.0).astype(BF16)
+
+    def own_body(m, carry):
+        for half, value in enumerate(split(leg_tri[m])):
+            mine = dot(value, pick)
+            leg_own_t[half, m] = mine.astype(BF16)
+            leg_own[half, m] = jnp.transpose(mine).astype(BF16)
         return carry
 
-    lax.fori_loop(0, tri_num, spread_body, 0)
-
-    def own_body(m, carry):
-        eighth, lane = m // SUB, lax.rem(m, SUB)
-        own = spread[pl.ds((eighth * lat_all + me * lat_loc) * SUB + lane, OWN, stride=SUB), :]
-        own = jnp.where(lax.broadcasted_iota(jnp.int32, (OWN, levels), 0) < lat_loc, own, 0.0)
-        leg_own[m] = own
-        leg_own_t[m] = jnp.transpose(own)[:tri_deg]
-        return carry
-
-    lax.fori_loop(0, tri_num, own_body, 0)
-
-    for b in range(CORES * blocks):
-        @pl.when(jnp.logical_and(is_full, core == b // blocks))
-        def _():
-            copy_tri(b, 3, mate).wait_recv()
-            copy_tri(b, 3, mate).start()
-    for b in range(CORES * blocks):
-        @pl.when(core != b // blocks)
-        def _():
-            copy_tri(b, 3, mate).wait_recv()
+    lax.fori_loop(0, tri_num, own_body, 0, unroll=4)
+
+    for b in range(CORES * blocks):
+        @pl.when(jnp.logical_and(jnp.logical_and(is_full, jnp.logical_not(forwards)), gets(b)))
+        def _():
+            copy_tri(b, 2, mate).wait_recv()
+            copy_tri(b, 2, mate).start()
+
+    for b in range(CORES * blocks):
+        @pl.when(jnp.logical_not(jnp.where(is_tri, core == b // blocks, gets(b))))
+        def _():
+            copy_tri(b, 2, mate).wait_recv()
 
     def tri_body(m, carry):
-        own_hi, own_lo = split(leg_own[m][:, :tri_deg])
+        own_hi, own_lo = leg_own[0, m], leg_own[1, m]
         c_hi, c_lo = split(jnp.concatenate([tri[m, 0], tri[m, 1]], axis=1))
         f = dot(own_hi, c_hi) + dot(own_lo, c_hi) + dot(own_hi, c_lo)
         for c in range(chunks):
@@ -260,7 +316,7 @@
             recv_a[rows(((c * group + full) * wave_loc + m) * SUB, SUB), :] = tile
         return carry
 
-    lax.fori_loop(0, tri_num, tri_body, 0)
+    lax.fori_loop(0, tri_num, tri_body, 0, unroll=4)
 
     for copy in mats[1:]:
         copy.wait()
@@ -305,19 +361,18 @@
                 def _():
                     copy_relay(dst, c).start()
 
-                @pl.when(jnp.logical_and(dst < full, jnp.logical_not(by_relay)))
+                late = jnp.logical_and(is_tri, lax.div(dst, CORES) == 1)
+
+                ready = jnp.logical_and(jnp.logical_or(jnp.logical_not(late), c >= LAG), jnp.logical_not(after_parts(dst, c)))
+
+                @pl.when(jnp.logical_and(jnp.logical_and(dst < full, jnp.logical_not(by_relay)), ready))
                 def _():
-                    copy_b(dst, c, 0, msg, recv_sem_b).start()
-
-        @pl.when(c == chunks - 1)
-        def _():
-            for g, start, size in starts(SIZES_B):
-                for off in order:
-                    dst = lax.rem(me + off, group)
-
-                    @pl.when(dst < full)
-                    def _():
-                        copy_b(dst, c, start * SUB, size * SUB, last_sem.at[g]).start()
+                    copy_b(dst, c, 0, msg, recv_sem_b.at[c]).start()
+
+                @pl.when(jnp.logical_and(late, c == LAG))
+                def _():
+                    for before in range(LAG):
+                        copy_b(dst, before, 0, msg, recv_sem_b.at[before]).start()
 
         @pl.when(is_full)
         def _():
@@ -326,27 +381,29 @@
     zero = jnp.zeros((SUB, levels), F32)
 
     def part_body(i, carry):
-        m = lax.rem(i + (1 - core) * wave_loc, tri_num)
+        side = jnp.where(i < wave_loc, 1 - core, core)
+        spread = BLOCK * (CORES * lax.div(lax.rem(i, wave_loc), BLOCK) + side) + lax.rem(i, BLOCK)
+        m = jnp.where(is_tri, lax.rem(i, wave_loc) + side * wave_loc, spread)
         re, im = [], []
         for t in range(OWN // SUB):
             a, b = (send_b[rows((c * waves + tri_m + m) * SUB, SUB), :] if c < chunks else zero for c in (2 * t, 2 * t + 1))
             re.append(jnp.where(low, a, pltpu.roll(b, QUAD, 0)))
             im.append(jnp.where(low, pltpu.roll(a, QUAD, 0), b))
         h_hi, h_lo = split(jnp.concatenate([jnp.concatenate(re, axis=0), jnp.concatenate(im, axis=0)], axis=1))
-        own_hi, own_lo = split(leg_own_t[m])
+        own_hi, own_lo = leg_own_t[0, m], leg_own_t[1, m]
         p_val = dot(own_hi, h_hi) + dot(own_lo, h_hi) + dot(own_hi, h_lo)
         part_own[m, 0] = p_val[:, :levels]
         part_own[m, 1] = p_val[:, levels:]
         return carry
 
-    lax.fori_loop(0, wave_loc, part_body, 0)
-    for b in range(CORES * blocks):
-        @pl.when(core != b // blocks)
+    lax.fori_loop(0, wave_loc, part_body, 0, unroll=4)
+    for b in range(CORES * blocks):
+        @pl.when(jnp.logical_not(keeps(b)))
         def _():
             copy_mate(b).start()
-    lax.fori_loop(wave_loc, tri_num, part_body, 0)
-    for b in range(CORES * blocks):
-        @pl.when(core == b // blocks)
+    lax.fori_loop(wave_loc, tri_num, part_body, 0, unroll=4)
+    for b in range(CORES * blocks):
+        @pl.when(keeps(b))
         def _():
             copy_mate(b).wait_recv()
 
@@ -354,10 +411,39 @@
             def _(i):
                 gap = skip(b)
                 for r in range(2):
-                    part_own[BLOCK * b + i, r, gap:, :] += part_mate[BLOCK * (b % blocks) + i, r, gap:, :]
-
-        @pl.when(jnp.logical_and(is_full, core == b // blocks))
-        def _():
+                    part_own[BLOCK * b + i, r, gap:, :] += part_mate[BLOCK * mate_slot(b) + i, r, gap:, :]
+
+        @pl.when(jnp.logical_and(jnp.logical_and(is_full, chip > 0), core == b % CORES))
+        def _():
+            copy_part(b).start()
+
+    for c in range(chunks - 1):
+        for off in order:
+            dst = lax.rem(me + off, group)
+
+            @pl.when(after_parts(dst, c))
+            def _():
+                copy_b(dst, c, 0, msg, recv_sem_b.at[c]).start()
+
+    for g, start, size in starts(SIZES_B):
+        for off in order:
+            dst = lax.rem(me + off, group)
+
+            @pl.when(dst < full)
+            def _():
+                copy_b(dst, chunks - 1, start * SUB, size * SUB, last_sem.at[g]).start()
+
+    for b in range(CORES * blocks):
+        @pl.when(jnp.logical_and(chip == 0, core == b % CORES))
+        def _():
+            gap = skip(b)
+            wait_part(b, 0)
+
+            @pl.loop(0, BLOCK)
+            def _(i):
+                for r in range(2):
+                    part_own[BLOCK * b + i, r, gap:, :] += part_in[0, BLOCK * (b % blocks) + i, r, gap:, :]
+
             copy_part(b).start()
 
     @pl.when(is_tri)
@@ -371,45 +457,60 @@
 
     @pl.when(is_full)
     def _():
-        wait_rows(recv_b, recv_sem_b, (chunks - 1) * (group - 1) * msg)
+        def add_up(m, parts, first):
+            re, im = [], []
+            for t in range(group * lat_loc // SUB):
+                tiles = []
+                for q in (2 * t, 2 * t + 1):
+                    src, c = divmod(q, chunks)
+                    tiles.append(recv_b[rows(((c * group + src) * wave_loc + m) * SUB, SUB), :] if c in parts else None)
+                a, b = tiles
+                if a is None and b is None:
+                    re.append(zero)
+                    im.append(zero)
+                    continue
+                a, b = (zero if x is None else x for x in (a, b))
+                re.append(jnp.where(low, a, pltpu.roll(b, QUAD, 0)))
+                im.append(jnp.where(low, pltpu.roll(a, QUAD, 0), b))
+            h_hi, h_lo = split(jnp.concatenate([jnp.concatenate(re, axis=0), jnp.concatenate(im, axis=0)], axis=1))
+            leg_hi, leg_lo = split(leg[m])
+            s_val = dot(leg_hi, h_hi) + dot(leg_lo, h_hi) + dot(leg_hi, h_lo)
+            for r in range(2):
+                value = s_val[:, r * levels:(r + 1) * levels]
+                spec[m, r] = value if first else spec[m, r] + value
+
+        for c in range(chunks - 2):
+                wait_rows(recv_b, recv_sem_b.at[c], (group - 1) * msg)
+
+        def early_body(m, carry):
+            add_up(m, range(chunks - 2), True)
+            return carry
+
+        lax.fori_loop(0, wave_loc, early_body, 0, unroll=2)
+        wait_rows(recv_b, recv_sem_b.at[chunks - 2], (group - 1) * msg)
         for g, start, size in starts(SIZES_B):
             wait_rows(recv_b, last_sem.at[g], (group - 1) * size * SUB)
 
-            def back_body(i, carry):
-                m = start + i
-                re, im = [], []
-                for t in range(group * lat_loc // SUB):
-                    tiles = []
-                    for q in (2 * t, 2 * t + 1):
-                        s, c = divmod(q, chunks)
-                        tiles.append(recv_b[rows(((c * group + s) * wave_loc + m) * SUB, SUB), :])
-                    a, b = tiles
-                    re.append(jnp.where(low, a, pltpu.roll(b, QUAD, 0)))
-                    im.append(jnp.where(low, pltpu.roll(a, QUAD, 0), b))
-                h_hi, h_lo = split(jnp.concatenate([jnp.concatenate(re, axis=0), jnp.concatenate(im, axis=0)], axis=1))
-                leg_hi, leg_lo = split(leg[m])
-                s_val = dot(leg_hi, h_hi) + dot(leg_lo, h_hi) + dot(leg_hi, h_lo)
-                spec[m, 0] = s_val[:, :levels]
-                spec[m, 1] = s_val[:, levels:]
+            def last_body(i, carry):
+                add_up(start + i, (chunks - 2, chunks - 1), False)
                 return carry
 
-            lax.fori_loop(0, size, back_body, 0)
+            lax.fori_loop(0, size, last_body, 0, unroll=2)
 
     for b in range(CORES * blocks):
         @pl.when(me == full + b // blocks)
         def _():
             gap = skip(b)
-            for src in range(chips - 1):
-                landed = part_in.at[src, pl.ds(BLOCK * (b % blocks), BLOCK), :, pl.ds(gap, tri_deg - gap), :]
-                pltpu.make_async_copy(landed, landed, part_recv.at[src, b]).wait()
+            for slot in range(2):
+                wait_part(b, slot)
 
             @pl.loop(0, BLOCK)
             def _(i):
                 m = BLOCK * (b % blocks) + i
                 for r in range(2):
                     acc = part_own[BLOCK * b + i, r, gap:, :]
-                    for src in range(chips - 1):
-                        acc = acc + part_in[src, m, r, gap:, :]
+                    for slot in range(2):
+                        acc = acc + part_in[slot, m, r, gap:, :]
                     spec[m, r, :tri_m + gap, :] = jnp.zeros((tri_m + gap, levels), F32)
                     spec[m, r, tri_m + gap:, :] = acc
 
@@ -424,20 +525,24 @@
         wait_rows(relay, relay_send, RELAYED * CORES * msg)
 
     for b in range(CORES * blocks):
-        @pl.when(core == b // blocks)
-        def _():
-            copy_tri(b, 3, mate).wait_send()
-
-        @pl.when(core != b // blocks)
+        @pl.when(jnp.where(is_tri, core == b // blocks, gets(b)))
+        def _():
+            copy_tri(b, 2, mate).wait_send()
+
+        @pl.when(jnp.logical_and(forwards, gets(b)))
+        def _():
+            copy_tri(b, 0, mate).wait_send()
+
+        @pl.when(jnp.logical_not(keeps(b)))
         def _():
             copy_mate(b).wait_send()
 
         @pl.when(me == full + b // blocks)
         def _():
-            for lane in range(3):
+            for lane in range(2):
                 copy_tri(b, lane, mate).wait_send()
 
-        @pl.when(jnp.logical_and(is_full, core == b // blocks))
+        @pl.when(jnp.logical_and(is_full, core == b % CORES))
         def _():
             copy_part(b).wait_send()
 
@@ -476,16 +581,15 @@
                 pltpu.VMEM((total, levels), F32),
                 pltpu.VMEM((tri_num, 2, tri_deg, levels), F32),
                 pltpu.VMEM((tri_num, tri_deg, legendre.shape[2]), F32),
-                pltpu.VMEM((tri_num * legendre.shape[2] + OWN * SUB, levels), F32),
-                pltpu.VMEM((tri_num, OWN, levels), F32),
-                pltpu.VMEM((tri_num, tri_deg, OWN), F32),
+                pltpu.VMEM((2, tri_num, OWN, tri_deg), BF16),
+                pltpu.VMEM((2, tri_num, tri_deg, OWN), BF16),
                 pltpu.VMEM((tri_num, 2, tri_deg, levels), F32),
                 pltpu.VMEM((wave_loc, 2, tri_deg, levels), F32),
-                pltpu.VMEM((group // CORES - 1, wave_loc, 2, tri_deg, levels), F32),
+                pltpu.VMEM((2, wave_loc, 2, tri_deg, levels), F32),
                 pltpu.VMEM((RELAYED * CORES * wave_loc * SUB, levels), F32),
-                dma((2, len(SIZES_A))), dma((3,)), dma, dma((lat_loc // QUAD,)), dma, dma, dma((len(SIZES_B),)),
-                dma((blocks,)), dma((4, blocks // CORES)), dma((blocks,)), dma((blocks,)), dma((blocks,)),
-                dma((blocks,)), dma((group // CORES - 1, blocks)), dma, dma((RELAYED * CORES,)),
+                dma((2, len(SIZES_A))), dma((3,)), dma, dma((lat_loc // QUAD,)), dma, dma((lat_loc // QUAD,)), dma((len(SIZES_B),)),
+                dma((blocks,)), dma((3, blocks)), dma((blocks,)), dma((blocks,)), dma((blocks,)),
+                dma((blocks,)), dma((2, blocks)), dma, dma((RELAYED * CORES,)),
             ],
             compiler_params=pltpu.CompilerParams(collective_id=0, has_side_effects=True, vmem_limit_bytes=48 * 2**20),
             name='transform_pair',

time: 82.4 us -> 79.5 us (0.965)
  the two profiles are of different devices: /device:TPU:112 before, /device:TPU:113 now
where the time goes in v4:
time: 79.5 us; the launch traced here: 78.5 us
  Pallas kernels  74.4 us (94%)
  local copies, waits for them, and re-layouts  3.42 us (4%)
    pallas_call x1, Pallas kernels, per_device(): pl.pallas_call(functools.partial(kernel, dims), out_shape=(pltpu.VMEM((la...  74.4 us
    unnamed x2, local copies, waits for them, and re-layouts  3.42 us

profile of v4, /device:TPU:113, one launch (start us, length us, event | category | flops | bytes accessed | tf_op | source)
XLA Modules:
  0.0 78.5 jit_solution(10637762226184169629)
XLA Ops:
  0.6 74.4 %transform_pair.1 = (f32[20,320,128]{2,1,0:T(8,128)S(1)}, f32[20,2,160,128]{3,2,1,0:T(8,128)S(1)}) custom-call(f32[20,2,160,128]{3,2,1,0:T(8,128)} %bitcast.5, f32[160,160,160]{2,1,0:T(8,128)} %leg_hbm.1, bf16[320,960]{1,0:T(8,128)(2,1)} %constant.4.clone.inv_hbm, bf16[320,960]{1,0:T(8,128)(2,1)} %constant.5.clone.fwd_hbm, f32[160]{0:T(256)} %wt_ref.1), custom_call_target="tpu_custom_call" | custom-call | tf_op jit(solution)/shard_map/transform_pair/pallas_call | solution.py:568
  75.1 1.7 %copy.9 = f32[128,20,320]{0,2,1:T(8,128)} copy(f32[128,20,320]{0,2,1:T(8,128)S(1)} %bitcast.4) | data formatting | bytes 6553600
  76.8 1.7 %copy.10 = f32[20,2,128,160]{2,3,1,0:T(8,128)} copy(f32[20,2,128,160]{2,3,1,0:T(8,128)S(1)} %bitcast.3) | data formatting | bytes 6553600

commit v5 on v4

--- a/solution.py
+++ b/solution.py
@@ -18,6 +18,7 @@
 SIZES_B = (8, 6, 4, 2)
 CORES = 2
 BLOCK = 4
+PIECES = 5
 OWN = 32
 HELD = 2
 LAG = 2
@@ -45,6 +46,14 @@
     return out
 
 
+def latitude_picks(group, lat_loc, first, num):
+    row = np.arange(group * lat_loc)
+    col = ((np.arange(group) * lat_loc)[None, :, None] + ((first + np.arange(num)) * QUAD)[:, None, None] + np.arange(QUAD)).reshape(-1)
+    one = (row[:, None] == col[None, :]).astype(ml_dtypes.bfloat16)
+    none = np.zeros_like(one)
+    return np.stack([np.concatenate([one, one, none], axis=1), np.concatenate([none, none, one], axis=1)])
+
+
 def split(x):
     hi = x.astype(BF16)
     lo = (x - hi.astype(F32)).astype(BF16)
@@ -55,9 +64,21 @@
     return lax.dot_general(a, b, (dims, ((), ())), preferred_element_type=F32)
 
 
-def kernel(dims, coef_hbm, leg_hbm, inv_hbm, fwd_hbm, wt_ref, grid, spec,
-           coef, leg, inv, fwd, send_a, recv_a, send_b, recv_b,
-           tri, leg_tri, leg_own, leg_own_t, part_own, part_mate, part_in, relay,
+def sums(recv, mine, m, parts, group, wave_loc, levels):
+    low = lax.broadcasted_iota(jnp.int32, (SUB, levels), 0) < QUAD
+    re, im = [], []
+    for c in parts:
+        for src in range(0, group, 2):
+            a, b = (recv[pl.ds(pl.multiple_of(((c * group + src + u) * wave_loc + m) * SUB, SUB), SUB), :] for u in range(2))
+            re.append(jnp.where(low, a, pltpu.roll(b, QUAD, 0)))
+            im.append(jnp.where(low, pltpu.roll(a, QUAD, 0), b))
+    h_hi, h_lo = split(jnp.concatenate([jnp.concatenate(re, axis=0), jnp.concatenate(im, axis=0)], axis=1))
+    return dot(mine, jnp.concatenate([h_hi, h_lo, h_hi], axis=0))
+
+
+def kernel(dims, coef_hbm, leg_hbm, inv_hbm, fwd_hbm, pick_early_hbm, pick_last_hbm, wt_ref, grid, spec, recv_b, leg_last,
+           coef, leg, inv, fwd, send_a, recv_a, send_b,
+           tri, leg_tri, leg_own, leg_own_t, part_own, part_mate, part_in, relay, pick_early, pick_last, leg_early,
            load_sem, mat_sem, send_sem_a, recv_sem_a, send_sem_b, recv_sem_b, last_sem,
            tri_load, tri_send, tri_recv, mate_send, mate_recv, part_send, part_recv, relay_send, relay_recv):
     group, wave_loc, levels, degs, lat_loc, waves, lon = dims
@@ -119,7 +140,8 @@
             load_block(b).start()
 
     leg_tri_copy = pltpu.make_async_copy(leg_hbm.at[pl.ds(tri_m, tri_num), pl.ds(tri_m, tri_deg), :], leg_tri, mat_sem.at[2])
-    mats = [leg_tri_copy, pltpu.make_async_copy(inv_hbm, inv, mat_sem.at[0]), pltpu.make_async_copy(fwd_hbm, fwd, mat_sem.at[1])]
+    mats = [leg_tri_copy, pltpu.make_async_copy(inv_hbm, inv, mat_sem.at[0]), pltpu.make_async_copy(fwd_hbm, fwd, mat_sem.at[1]),
+            pltpu.make_async_copy(pick_early_hbm, pick_early, mat_sem.at[3]), pltpu.make_async_copy(pick_last_hbm, pick_last, mat_sem.at[4])]
     for copy in mats:
         copy.start()
 
@@ -433,6 +455,16 @@
             def _():
                 copy_b(dst, chunks - 1, start * SUB, size * SUB, last_sem.at[g]).start()
 
+    @pl.when(is_full)
+    def _():
+        def pick_body(m, carry):
+            leg_hi, leg_lo = split(leg[m])
+            leg_early[m] = (dot(leg_hi, pick_early[0]) + dot(leg_lo, pick_early[1])).astype(BF16)
+            leg_last[m] = (dot(leg_hi, pick_last[0]) + dot(leg_lo, pick_last[1])).astype(BF16)
+            return carry
+
+        lax.fori_loop(0, wave_loc, pick_body, 0, unroll=2)
+
     for b in range(CORES * blocks):
         @pl.when(jnp.logical_and(chip == 0, core == b % CORES))
         def _():
@@ -457,45 +489,19 @@
 
     @pl.when(is_full)
     def _():
-        def add_up(m, parts, first):
-            re, im = [], []
-            for t in range(group * lat_loc // SUB):
-                tiles = []
-                for q in (2 * t, 2 * t + 1):
-                    src, c = divmod(q, chunks)
-                    tiles.append(recv_b[rows(((c * group + src) * wave_loc + m) * SUB, SUB), :] if c in parts else None)
-                a, b = tiles
-                if a is None and b is None:
-                    re.append(zero)
-                    im.append(zero)
-                    continue
-                a, b = (zero if x is None else x for x in (a, b))
-                re.append(jnp.where(low, a, pltpu.roll(b, QUAD, 0)))
-                im.append(jnp.where(low, pltpu.roll(a, QUAD, 0), b))
-            h_hi, h_lo = split(jnp.concatenate([jnp.concatenate(re, axis=0), jnp.concatenate(im, axis=0)], axis=1))
-            leg_hi, leg_lo = split(leg[m])
-            s_val = dot(leg_hi, h_hi) + dot(leg_lo, h_hi) + dot(leg_hi, h_lo)
-            for r in range(2):
-                value = s_val[:, r * levels:(r + 1) * levels]
-                spec[m, r] = value if first else spec[m, r] + value
-
         for c in range(chunks - 2):
                 wait_rows(recv_b, recv_sem_b.at[c], (group - 1) * msg)
 
         def early_body(m, carry):
-            add_up(m, range(chunks - 2), True)
+            s_val = sums(recv_b, leg_early[m], m, range(chunks - 2), group, wave_loc, levels)
+            for r in range(2):
+                spec[m, r] = s_val[:, r * levels:(r + 1) * levels]
             return carry
 
         lax.fori_loop(0, wave_loc, early_body, 0, unroll=2)
         wait_rows(recv_b, recv_sem_b.at[chunks - 2], (group - 1) * msg)
         for g, start, size in starts(SIZES_B):
             wait_rows(recv_b, last_sem.at[g], (group - 1) * size * SUB)
-
-            def last_body(i, carry):
-                add_up(start + i, (chunks - 2, chunks - 1), False)
-                return carry
-
-            lax.fori_loop(0, size, last_body, 0, unroll=2)
 
     for b in range(CORES * blocks):
         @pl.when(me == full + b // blocks)
@@ -545,6 +551,40 @@
         @pl.when(jnp.logical_and(is_full, core == b % CORES))
         def _():
             copy_part(b).wait_send()
+
+
+def finish(dims, grid, early, recv_b, leg_last, grid_hbm, spec_hbm, spec, grid_sem, spec_sem):
+    group, wave_loc, levels, degs, lat_loc, waves, lon = dims
+    chunks = lat_loc // QUAD
+    is_full = lax.axis_index('w') < group - CORES
+    copies = []
+    for p in range(PIECES):
+        part = pl.ds(p * (lat_loc // PIECES), lat_loc // PIECES)
+        copies.append(pltpu.make_async_copy(grid.at[part], grid_hbm.at[part], grid_sem.at[p]))
+        copies[-1].start()
+    size = wave_loc // PIECES
+    for p in range(PIECES):
+        part = pl.ds(p * size, size)
+
+        @pl.when(is_full)
+        def _():
+            def last_body(i, carry):
+                m = p * size + i
+                s_val = sums(recv_b, leg_last[m], m, (chunks - 2, chunks - 1), group, wave_loc, levels)
+                for r in range(2):
+                    spec[m, r] = early[m, r] + s_val[:, r * levels:(r + 1) * levels]
+                return carry
+
+            lax.fori_loop(0, size, last_body, 0, unroll=4)
+            pltpu.make_async_copy(spec.at[part], spec_hbm.at[part], spec_sem.at[p]).start()
+
+        @pl.when(jnp.logical_not(is_full))
+        def _():
+            pltpu.make_async_copy(early.at[part], spec_hbm.at[part], spec_sem.at[p]).start()
+
+        copies.append(pltpu.make_async_copy(spec.at[part], spec_hbm.at[part], spec_sem.at[p]))
+    for copy in copies:
+        copy.wait()
 
 
 def solution(mesh):
@@ -560,22 +600,24 @@
         tri_num = CORES * wave_loc
         tri_deg = degs - waves + tri_num
         blocks = tri_num // BLOCK
+        chunks = lat_loc // QUAD
+        pick_early = jnp.asarray(latitude_picks(group, lat_loc, 0, chunks - 2))
+        pick_last = jnp.asarray(latitude_picks(group, lat_loc, chunks - 2, 2))
         total = group * lat_loc // QUAD * wave_loc * SUB
         dims = (group, wave_loc, levels, degs, lat_loc, waves, lon)
-        hbm = pl.BlockSpec(memory_space=pl.ANY)
+        hbm = pl.BlockSpec(memory_space=pltpu.HBM)
         vmem = pl.BlockSpec(memory_space=pltpu.VMEM)
         dma = pltpu.SemaphoreType.DMA
-        grid, spec = pl.pallas_call(
+        grid, spec, recv_b, leg_last = pl.pallas_call(
             functools.partial(kernel, dims),
-            out_shape=(pltpu.VMEM((lat_loc, lon, levels), F32), pltpu.VMEM(coef_t.shape, F32)),
-            in_specs=[hbm, hbm, hbm, hbm, pl.BlockSpec(memory_space=pltpu.SMEM)],
-            out_specs=(vmem, vmem),
+            out_shape=(pltpu.VMEM((lat_loc, lon, levels), F32), pltpu.VMEM(coef_t.shape, F32), pltpu.VMEM((total, levels), F32), pltpu.VMEM((wave_loc, degs, pick_last.shape[2]), BF16)),
+            in_specs=[hbm, hbm, hbm, hbm, hbm, hbm, pl.BlockSpec(memory_space=pltpu.SMEM)],
+            out_specs=(vmem, vmem, vmem, vmem),
             scratch_shapes=[
                 pltpu.VMEM(coef_t.shape, F32),
                 pltpu.VMEM((wave_loc, degs, legendre.shape[2]), F32),
                 pltpu.VMEM(inv.shape, BF16),
                 pltpu.VMEM(fwd.shape, BF16),
-                pltpu.VMEM((total, levels), F32),
                 pltpu.VMEM((total, levels), F32),
                 pltpu.VMEM((total, levels), F32),
                 pltpu.VMEM((total, levels), F32),
@@ -587,13 +629,25 @@
                 pltpu.VMEM((wave_loc, 2, tri_deg, levels), F32),
                 pltpu.VMEM((2, wave_loc, 2, tri_deg, levels), F32),
                 pltpu.VMEM((RELAYED * CORES * wave_loc * SUB, levels), F32),
-                dma((2, len(SIZES_A))), dma((3,)), dma, dma((lat_loc // QUAD,)), dma, dma((lat_loc // QUAD,)), dma((len(SIZES_B),)),
+                pltpu.VMEM(pick_early.shape, BF16),
+                pltpu.VMEM(pick_last.shape, BF16),
+                pltpu.VMEM((wave_loc, degs, pick_early.shape[2]), BF16),
+                dma((2, len(SIZES_A))), dma((5,)), dma, dma((lat_loc // QUAD,)), dma, dma((lat_loc // QUAD,)), dma((len(SIZES_B),)),
                 dma((blocks,)), dma((3, blocks)), dma((blocks,)), dma((blocks,)), dma((blocks,)),
                 dma((blocks,)), dma((2, blocks)), dma, dma((RELAYED * CORES,)),
             ],
-            compiler_params=pltpu.CompilerParams(collective_id=0, has_side_effects=True, vmem_limit_bytes=48 * 2**20),
+            compiler_params=pltpu.CompilerParams(collective_id=0, has_side_effects=True, vmem_limit_bytes=52 * 2**20),
             name='transform_pair',
-        )(coef_t, legendre, inv, fwd, gauss_weight)
+        )(coef_t, legendre, inv, fwd, pick_early, pick_last, gauss_weight)
+        grid, spec = pl.pallas_call(
+            functools.partial(finish, dims),
+            out_shape=(jax.ShapeDtypeStruct(grid.shape, F32), jax.ShapeDtypeStruct(spec.shape, F32)),
+            in_specs=[vmem, vmem, vmem, vmem],
+            out_specs=(hbm, hbm),
+            scratch_shapes=[pltpu.VMEM(spec.shape, F32), dma((PIECES,)), dma((PIECES,))],
+            compiler_params=pltpu.CompilerParams(vmem_limit_bytes=8 * 2**20),
+            name='finish',
+        )(grid, spec, recv_b, leg_last)
         return jnp.transpose(grid, (2, 0, 1)), jnp.transpose(spec, (0, 1, 3, 2))
 
     return jax.shard_map(per_device, mesh=mesh, in_specs=(P('w', None, 'lev', None), P(None, None, None), P(None)), out_specs=(P('lev', 'w', None), P('w', None, 'lev', None)), check_vma=False)

time: 79.5 us -> 77 us (0.969); the launches traced: 78.5 us -> 76.9 us
  local copies, waits for them, and re-layouts: 3.42 us -> 0 us
  Pallas kernels: 74.4 us -> 76.3 us
    unnamed x2 -> x0, local copies, waits for them, and re-layouts: 3.42 us -> none
    pallas_call x0 -> x1, Pallas kernels: none -> 2.83 us  [per_device(): pl.pallas_call(functools.partial(finish, dims), out_shape=(jax.ShapeDtype...]
    pallas_call x1, Pallas kernels: 74.4 us -> 73.5 us  [per_device(): pl.pallas_call(functools.partial(kernel, dims), out_shape=(pltpu.VMEM((la...]
where the time goes in v5:
time: 77 us; the launch traced here: 76.9 us
  Pallas kernels  76.3 us (99%)
    pallas_call x1, Pallas kernels, per_device(): pl.pallas_call(functools.partial(kernel, dims), out_shape=(pltpu.VMEM((la...  73.5 us
    pallas_call x1, Pallas kernels, per_device(): pl.pallas_call(functools.partial(finish, dims), out_shape=(jax.ShapeDtype...  2.83 us

profile of v5, /device:TPU:113, one launch (start us, length us, event | category | flops | bytes accessed | tf_op | source)
XLA Modules:
  0.0 76.9 jit_solution(12380162540021365009)
XLA Ops:
  0.6 73.5 %transform_pair.1 = (f32[20,320,128]{2,1,0:T(8,128)S(1)}, f32[20,2,160,128]{3,2,1,0:T(8,128)S(1)}, f32[6400,128]{1,0:T(8,128)S(1)}, bf16[20,160,192]{2,1,0:T(8,128)(2,1)S(1)}) custom-call(f32[20,2,160,128]{3,2,1,0:T(8,128)} %bitcast.3, f32[160,160,160]{2,1,0:T(8,128)} %leg_hbm.1, bf16[320,960]{1,0:T(8,128)(2,1)} %constant.8.clone.inv_hbm, ...), custom_call_target="tpu_custom_call" | custom-call | tf_op jit(solution)/shard_map/transform_pair/pallas_call | solution.py:611
  74.1 2.8 %finish.1 = (f32[20,320,128]{2,1,0:T(8,128)}, f32[20,2,160,128]{3,2,1,0:T(8,128)}) custom-call(f32[20,320,128]{2,1,0:T(8,128)S(1)} %get-tuple-element.8.grid, f32[20,2,160,128]{3,2,1,0:T(8,128)S(1)} %get-tuple-element.9.early, f32[6400,128]{1,0:T(8,128)S(1)} %get-tuple-element.10.recv_b, bf16[20,160,192]{2,1,0:T(8,128)(2,1)S(1)} %get-tuple-element.11.leg_last), custom_call_target="tpu_custom_call" | custom-call | tf_op jit(solution)/shard_map/finish/pallas_call | solution.py:642

commit v6 on v5

--- a/solution.py
+++ b/solution.py
@@ -13,9 +13,8 @@
 F32, BF16 = jnp.float32, jnp.bfloat16
 SUB = 8
 QUAD = 4
-SIZES_A = (4, 4, 4, 8)
+SIZES_A = (2, 6, 4, 8)
 EARLY = 2
-SIZES_B = (8, 6, 4, 2)
 CORES = 2
 BLOCK = 4
 PIECES = 5
@@ -79,8 +78,8 @@
 def kernel(dims, coef_hbm, leg_hbm, inv_hbm, fwd_hbm, pick_early_hbm, pick_last_hbm, wt_ref, grid, spec, recv_b, leg_last,
            coef, leg, inv, fwd, send_a, recv_a, send_b,
            tri, leg_tri, leg_own, leg_own_t, part_own, part_mate, part_in, relay, pick_early, pick_last, leg_early,
-           load_sem, mat_sem, send_sem_a, recv_sem_a, send_sem_b, recv_sem_b, last_sem,
-           tri_load, tri_send, tri_recv, mate_send, mate_recv, part_send, part_recv, relay_send, relay_recv):
+           load_sem, mat_sem, send_sem_a, recv_sem_a, send_sem_b, recv_sem_b,
+           tri_load, tri_recv, mate_recv, part_recv, relay_recv, misc_send):
     group, wave_loc, levels, degs, lat_loc, waves, lon = dims
     chunks = lat_loc // QUAD
     msg = wave_loc * SUB
@@ -126,7 +125,7 @@
         gap = skip(b)
         return pltpu.make_async_copy(
             coef_hbm.at[pl.ds(BLOCK * (b % blocks), BLOCK), :, pl.ds(tri_m + gap, tri_deg - gap), :],
-            tri.at[pl.ds(BLOCK * b, BLOCK), :, pl.ds(gap, tri_deg - gap), :], tri_load.at[b])
+            tri.at[pl.ds(BLOCK * b, BLOCK), :, pl.ds(gap, tri_deg - gap), :], tri_load.at[b % blocks])
 
     @pl.when(is_full)
     def _():
@@ -173,13 +172,13 @@
         slot = c * CORES + e
         return pltpu.make_async_remote_copy(
             src_ref=relay.at[rows(slot * msg, msg)], dst_ref=recv_b.at[rows((c * group + core) * msg, msg)],
-            send_sem=relay_send, recv_sem=recv_sem_b.at[c], device_id={'w': group // 2 + e}, device_id_type=MESH)
-
-    def copy_tri(b, lane, dst):
+            send_sem=misc_send, recv_sem=recv_sem_b.at[c], device_id={'w': group // 2 + e}, device_id_type=MESH)
+
+    def copy_tri(b, dst):
         gap = skip(b)
         ref = tri.at[pl.ds(BLOCK * b, BLOCK), :, pl.ds(gap, tri_deg - gap), :]
         return pltpu.make_async_remote_copy(
-            src_ref=ref, dst_ref=ref, send_sem=tri_send.at[lane, b], recv_sem=tri_recv.at[b],
+            src_ref=ref, dst_ref=ref, send_sem=misc_send, recv_sem=tri_recv.at[b],
             device_id={'w': dst}, device_id_type=MESH)
 
     def entry(b, at):
@@ -199,7 +198,7 @@
         return pltpu.make_async_remote_copy(
             src_ref=part_own.at[pl.ds(BLOCK * b, BLOCK), :, pl.ds(gap, tri_deg - gap), :],
             dst_ref=part_mate.at[pl.ds(BLOCK * mate_slot(b), BLOCK), :, pl.ds(gap, tri_deg - gap), :],
-            send_sem=mate_send.at[b], recv_sem=mate_recv.at[b], device_id={'w': mate}, device_id_type=MESH)
+            send_sem=misc_send, recv_sem=mate_recv.at[mate_slot(b)], device_id={'w': mate}, device_id_type=MESH)
 
     def copy_part(b):
         gap = skip(b)
@@ -209,12 +208,12 @@
         return pltpu.make_async_remote_copy(
             src_ref=part_own.at[pl.ds(BLOCK * b, BLOCK), :, pl.ds(gap, tri_deg - gap), :],
             dst_ref=part_in.at[slot, pl.ds(BLOCK * (b % blocks), BLOCK), :, pl.ds(gap, tri_deg - gap), :],
-            send_sem=part_send.at[b], recv_sem=part_recv.at[slot, b], device_id={'w': dst}, device_id_type=MESH)
+            send_sem=misc_send, recv_sem=part_recv.at[slot, b % blocks], device_id={'w': dst}, device_id_type=MESH)
 
     def wait_part(b, slot):
         gap = skip(b)
         landed = part_in.at[slot, pl.ds(BLOCK * (b % blocks), BLOCK), :, pl.ds(gap, tri_deg - gap), :]
-        pltpu.make_async_copy(landed, landed, part_recv.at[slot, b]).wait()
+        pltpu.make_async_copy(landed, landed, part_recv.at[slot, b % blocks]).wait()
 
     def wait_rows(ref, sem, count):
         landed = ref.at[pl.ds(0, count)]
@@ -225,7 +224,7 @@
 
     def held(off, c):
         dst_chip = lax.div(lax.rem(me + off, group), CORES)
-        return jnp.logical_and(forwards, jnp.logical_or(dst_chip == 0, jnp.logical_and(dst_chip == 1, c >= HELD)))
+        return jnp.logical_and(jnp.logical_and(forwards, dst_chip == 1), c >= HELD)
 
     @pl.when(is_full)
     def _():
@@ -280,17 +279,17 @@
             @pl.when(core == b // blocks)
             def _():
                 load_block(b).wait()
-                for lane, dst in enumerate([full - CORES + entry(b, chips - 2), entry(b, 0), mate]):
-                    copy_tri(b, lane, dst).start()
+                for dst in (full - CORES + entry(b, chips - 2), entry(b, 0), mate):
+                    copy_tri(b, dst).start()
 
     @pl.when(forwards)
     def _():
         for b in range(CORES * blocks):
             @pl.when(gets(b))
             def _():
-                copy_tri(b, 2, mate).wait_recv()
-                copy_tri(b, 0, full - 2 * CORES + entry(b, 1)).start()
-                copy_tri(b, 2, mate).start()
+                copy_tri(b, mate).wait_recv()
+                copy_tri(b, full - 2 * CORES + entry(b, 1)).start()
+                copy_tri(b, mate).start()
 
         @pl.loop(1, chunks)
         def _(c):
@@ -318,13 +317,13 @@
     for b in range(CORES * blocks):
         @pl.when(jnp.logical_and(jnp.logical_and(is_full, jnp.logical_not(forwards)), gets(b)))
         def _():
-            copy_tri(b, 2, mate).wait_recv()
-            copy_tri(b, 2, mate).start()
+            copy_tri(b, mate).wait_recv()
+            copy_tri(b, mate).start()
 
     for b in range(CORES * blocks):
         @pl.when(jnp.logical_not(jnp.where(is_tri, core == b // blocks, gets(b))))
         def _():
-            copy_tri(b, 2, mate).wait_recv()
+            copy_tri(b, mate).wait_recv()
 
     def tri_body(m, carry):
         own_hi, own_lo = leg_own[0, m], leg_own[1, m]
@@ -447,13 +446,12 @@
             def _():
                 copy_b(dst, c, 0, msg, recv_sem_b.at[c]).start()
 
-    for g, start, size in starts(SIZES_B):
-        for off in order:
-            dst = lax.rem(me + off, group)
-
-            @pl.when(dst < full)
-            def _():
-                copy_b(dst, chunks - 1, start * SUB, size * SUB, last_sem.at[g]).start()
+    for off in order:
+        dst = lax.rem(me + off, group)
+
+        @pl.when(dst < full)
+        def _():
+            copy_b(dst, chunks - 1, 0, msg, recv_sem_b.at[chunks - 1]).start()
 
     @pl.when(is_full)
     def _():
@@ -499,9 +497,8 @@
             return carry
 
         lax.fori_loop(0, wave_loc, early_body, 0, unroll=2)
-        wait_rows(recv_b, recv_sem_b.at[chunks - 2], (group - 1) * msg)
-        for g, start, size in starts(SIZES_B):
-            wait_rows(recv_b, last_sem.at[g], (group - 1) * size * SUB)
+        for c in range(chunks - 2, chunks):
+            wait_rows(recv_b, recv_sem_b.at[c], (group - 1) * msg)
 
     for b in range(CORES * blocks):
         @pl.when(me == full + b // blocks)
@@ -528,29 +525,23 @@
     @pl.when(is_tri)
     def _():
         wait_rows(send_b, send_sem_b, full * chunks * msg)
-        wait_rows(relay, relay_send, RELAYED * CORES * msg)
-
-    for b in range(CORES * blocks):
-        @pl.when(jnp.where(is_tri, core == b // blocks, gets(b)))
-        def _():
-            copy_tri(b, 2, mate).wait_send()
-
-        @pl.when(jnp.logical_and(forwards, gets(b)))
-        def _():
-            copy_tri(b, 0, mate).wait_send()
-
-        @pl.when(jnp.logical_not(keeps(b)))
-        def _():
-            copy_mate(b).wait_send()
-
-        @pl.when(me == full + b // blocks)
-        def _():
-            for lane in range(2):
-                copy_tri(b, lane, mate).wait_send()
-
-        @pl.when(jnp.logical_and(is_full, core == b % CORES))
-        def _():
-            copy_part(b).wait_send()
+
+    def block_rows(blks):
+        return sum(BLOCK * 2 * (tri_deg - skip(b)) for b in blks)
+
+    for at in range(chips):
+        for p in range(CORES):
+            if at == chips - 1:
+                own = [b for b in range(CORES * blocks) if b // blocks == p]
+                mates = [b for b in range(CORES * blocks) if b // blocks != p]
+                count = 3 * block_rows(own) + block_rows(mates) + RELAYED * CORES * msg
+            else:
+                come = [b for b in range(CORES * blocks) if entry(b, at) == p]
+                count = block_rows(come) * (2 if at == chips - 2 else 1) + block_rows(range(CORES * blocks))
+
+            @pl.when(jnp.logical_and(chip == at, core == p))
+            def _():
+                wait_rows(send_a, misc_send, count)
 
 
 def finish(dims, grid, early, recv_b, leg_last, grid_hbm, spec_hbm, spec, grid_sem, spec_sem):
@@ -632,9 +623,8 @@
                 pltpu.VMEM(pick_early.shape, BF16),
                 pltpu.VMEM(pick_last.shape, BF16),
                 pltpu.VMEM((wave_loc, degs, pick_early.shape[2]), BF16),
-                dma((2, len(SIZES_A))), dma((5,)), dma, dma((lat_loc // QUAD,)), dma, dma((lat_loc // QUAD,)), dma((len(SIZES_B),)),
-                dma((blocks,)), dma((3, blocks)), dma((blocks,)), dma((blocks,)), dma((blocks,)),
-                dma((blocks,)), dma((2, blocks)), dma, dma((RELAYED * CORES,)),
+                dma((2, len(SIZES_A))), dma((5,)), dma, dma((lat_loc // QUAD,)), dma, dma((lat_loc // QUAD,)),
+                dma((blocks // CORES,)), dma((blocks,)), dma((blocks // CORES,)), dma((2, blocks // CORES)), dma((RELAYED * CORES,)), dma,
             ],
             compiler_params=pltpu.CompilerParams(collective_id=0, has_side_effects=True, vmem_limit_bytes=52 * 2**20),
             name='transform_pair',

time: 77 us -> 75 us (0.974)
  Pallas kernels: 76.3 us -> 74.2 us
    pallas_call x1, Pallas kernels: 73.5 us -> 71.4 us  [per_device(): pl.pallas_call(functools.partial(kernel, dims), out_shape=(pltpu.VMEM((la...]
where the time goes in v6:
time: 75 us; the launch traced here: 74.9 us
  Pallas kernels  74.2 us (99%)
    pallas_call x1, Pallas kernels, per_device(): pl.pallas_call(functools.partial(kernel, dims), out_shape=(pltpu.VMEM((la...  71.4 us
    pallas_call x1, Pallas kernels, per_device(): pl.pallas_call(functools.partial(finish, dims), out_shape=(jax.ShapeDtype...  2.83 us

profile of v6, /device:TPU:113, one launch (start us, length us, event | category | flops | bytes accessed | tf_op | source)
XLA Modules:
  0.0 74.9 jit_solution(3882999315380927217)
XLA Ops:
  0.6 71.4 %transform_pair.1 = (f32[20,320,128]{2,1,0:T(8,128)S(1)}, f32[20,2,160,128]{3,2,1,0:T(8,128)S(1)}, f32[6400,128]{1,0:T(8,128)S(1)}, bf16[20,160,192]{2,1,0:T(8,128)(2,1)S(1)}) custom-call(f32[20,2,160,128]{3,2,1,0:T(8,128)} %bitcast.3, f32[160,160,160]{2,1,0:T(8,128)} %leg_hbm.1, bf16[320,960]{1,0:T(8,128)(2,1)} %constant.8.clone.inv_hbm, ...), custom_call_target="tpu_custom_call" | custom-call | tf_op jit(solution)/shard_map/transform_pair/pallas_call | solution.py:602
  72.0 2.8 %finish.1 = (f32[20,320,128]{2,1,0:T(8,128)}, f32[20,2,160,128]{3,2,1,0:T(8,128)}) custom-call(f32[20,320,128]{2,1,0:T(8,128)S(1)} %get-tuple-element.8.grid, f32[20,2,160,128]{3,2,1,0:T(8,128)S(1)} %get-tuple-element.9.early, f32[6400,128]{1,0:T(8,128)S(1)} %get-tuple-element.10.recv_b, bf16[20,160,192]{2,1,0:T(8,128)(2,1)S(1)} %get-tuple-element.11.leg_last), custom_call_target="tpu_custom_call" | custom-call | tf_op jit(solution)/shard_map/finish/pallas_call | solution.py:632

commit v7 on v6

--- a/solution.py
+++ b/solution.py
@@ -79,7 +79,7 @@
            coef, leg, inv, fwd, send_a, recv_a, send_b,
            tri, leg_tri, leg_own, leg_own_t, part_own, part_mate, part_in, relay, pick_early, pick_last, leg_early,
            load_sem, mat_sem, send_sem_a, recv_sem_a, send_sem_b, recv_sem_b,
-           tri_load, tri_recv, mate_recv, part_recv, relay_recv, misc_send):
+           tri_recv, mate_recv, part_recv, misc_send):
     group, wave_loc, levels, degs, lat_loc, waves, lon = dims
     chunks = lat_loc // QUAD
     msg = wave_loc * SUB
@@ -125,7 +125,7 @@
         gap = skip(b)
         return pltpu.make_async_copy(
             coef_hbm.at[pl.ds(BLOCK * (b % blocks), BLOCK), :, pl.ds(tri_m + gap, tri_deg - gap), :],
-            tri.at[pl.ds(BLOCK * b, BLOCK), :, pl.ds(gap, tri_deg - gap), :], tri_load.at[b % blocks])
+            tri.at[pl.ds(BLOCK * b, BLOCK), :, pl.ds(gap, tri_deg - gap), :], load_sem.at[b % blocks % 2, b % blocks // 2])
 
     @pl.when(is_full)
     def _():
@@ -166,7 +166,7 @@
         slot = c * CORES + lax.rem(dst, CORES)
         return pltpu.make_async_remote_copy(
             src_ref=send_b.at[rows((c * group + dst) * msg, msg)], dst_ref=relay.at[rows(slot * msg, msg)],
-            send_sem=send_sem_b, recv_sem=relay_recv.at[slot], device_id={'w': full + core}, device_id_type=MESH)
+            send_sem=send_sem_b, recv_sem=recv_sem_b.at[slot], device_id={'w': full + core}, device_id_type=MESH)
 
     def copy_onward(c, e):
         slot = c * CORES + e
@@ -482,7 +482,7 @@
             for e in range(CORES):
                 slot = c * CORES + e
                 landed = relay.at[pl.ds(slot * msg, msg)]
-                pltpu.make_async_copy(landed, landed, relay_recv.at[slot]).wait()
+                pltpu.make_async_copy(landed, landed, recv_sem_b.at[slot]).wait()
                 copy_onward(c, e).start()
 
     @pl.when(is_full)
@@ -624,7 +624,7 @@
                 pltpu.VMEM(pick_last.shape, BF16),
                 pltpu.VMEM((wave_loc, degs, pick_early.shape[2]), BF16),
                 dma((2, len(SIZES_A))), dma((5,)), dma, dma((lat_loc // QUAD,)), dma, dma((lat_loc // QUAD,)),
-                dma((blocks // CORES,)), dma((blocks,)), dma((blocks // CORES,)), dma((2, blocks // CORES)), dma((RELAYED * CORES,)), dma,
+                dma((blocks,)), dma((blocks // CORES,)), dma((2, blocks // CORES)), dma,
             ],
             compiler_params=pltpu.CompilerParams(collective_id=0, has_side_effects=True, vmem_limit_bytes=52 * 2**20),
             name='transform_pair',

time: 75 us -> 74.9 us (level)
  no operation moved by 1% of the time
where the time goes in v7:
time: 74.9 us; the launch traced here: 74.8 us
  Pallas kernels  74.2 us (99%)
    pallas_call x1, Pallas kernels, per_device(): pl.pallas_call(functools.partial(kernel, dims), out_shape=(pltpu.VMEM((la...  71.3 us
    pallas_call x1, Pallas kernels, per_device(): pl.pallas_call(functools.partial(finish, dims), out_shape=(jax.ShapeDtype...  2.83 us

profile of v7, /device:TPU:113, one launch (start us, length us, event | category | flops | bytes accessed | tf_op | source)
XLA Modules:
  0.0 74.8 jit_solution(15781298303385094875)
XLA Ops:
  0.6 71.3 %transform_pair.1 = (f32[20,320,128]{2,1,0:T(8,128)S(1)}, f32[20,2,160,128]{3,2,1,0:T(8,128)S(1)}, f32[6400,128]{1,0:T(8,128)S(1)}, bf16[20,160,192]{2,1,0:T(8,128)(2,1)S(1)}) custom-call(f32[20,2,160,128]{3,2,1,0:T(8,128)} %bitcast.3, f32[160,160,160]{2,1,0:T(8,128)} %leg_hbm.1, bf16[320,960]{1,0:T(8,128)(2,1)} %constant.8.clone.inv_hbm, ...), custom_call_target="tpu_custom_call" | custom-call | tf_op jit(solution)/shard_map/transform_pair/pallas_call | solution.py:602
  72.0 2.8 %finish.1 = (f32[20,320,128]{2,1,0:T(8,128)}, f32[20,2,160,128]{3,2,1,0:T(8,128)}) custom-call(f32[20,320,128]{2,1,0:T(8,128)S(1)} %get-tuple-element.8.grid, f32[20,2,160,128]{3,2,1,0:T(8,128)S(1)} %get-tuple-element.9.early, f32[6400,128]{1,0:T(8,128)S(1)} %get-tuple-element.10.recv_b, bf16[20,160,192]{2,1,0:T(8,128)(2,1)S(1)} %get-tuple-element.11.leg_last), custom_call_target="tpu_custom_call" | custom-call | tf_op jit(solution)/shard_map/finish/pallas_call | solution.py:632
